TPU v7x, 256 devices: a whole 4x4x8 slice. The times are simulated.
256 devices in a mesh: leaf: 8 (over z_hi, core), seq: 32 (over x, z_lo, y).
Axes of the slice: x: 4, y: 4, z: 8 (z_hi: 4, z_lo: 2; z = z_hi * 2 + z_lo), core: 2. Of those that a mesh axis runs over, the one named last changes fastest.
Arguments:
- queries: bfloat16 [8, 8192, 4096], P('leaf', 'seq'), may hold values from -40 to 40
- branch_key_rows: bfloat16 [8, 8192, 512], P('leaf', 'seq'), may hold values from -6 to 6
- branch_value_rows: bfloat16 [8, 8192, 512], P('leaf', 'seq'), may hold values from -6 to 6
- grad_output: bfloat16 [8, 8192, 4096], P('leaf', 'seq'), may hold values from -6 to 6
- trunk_keys: bfloat16 [8, 256, 512], P('leaf', 'seq'), may hold values from -6 to 6
- trunk_token_values: bfloat16 [8, 256, 512], P('leaf', 'seq'), may hold values from -6 to 6
- lengths: int32 [8, 128], P(None, 'seq'), may hold values from 0 to 64, as said below
- parents: int32 [8, 128], P(None, 'seq'), may hold values from 1 to 255
Outputs:
- grad_queries: float32 [8, 8192, 4096], P('leaf', 'seq')
- grad_branch_keys: float32 [8, 8192, 512], P('leaf', 'seq')
- grad_branch_values: float32 [8, 8192, 512], P('leaf', 'seq')
- grad_trunk_keys: float32 [8, 256, 512], P('leaf', 'seq')
- grad_trunk_values: float32 [8, 256, 512], P('leaf', 'seq')
Inputs may be any that keep to these rules, and one draw needn't show every extreme that they name: `lengths`: 0 means that the slot holds no branch.
All inputs are finite; a program needn't handle non-finite values.
Results may differ from a plain program's by a relative error of at most 0.0052.
Values may be sent and summed in bfloat16 or wider, within the bound.
No kernel may reach another device: no remote copies, remote signals or barrier semaphores. Data moves between devices by JAX's collectives and lax.ppermute only.
A program may use at most 64 MiB of HBM per device.

v0:
```python
import math

import jax
import jax.numpy as jnp
from jax import lax
from jax.sharding import PartitionSpec as P

HEAD_SIZE = 128


masked_score = -1e30


def partner_2(block, axis, stride):
    count = lax.axis_size(axis)
    route = []
    for low in range(count):
        high = low | 1 << stride
        if high != low and high < count:
            route += [(low, high), (high, low)]
    return lax.ppermute(block, axis, route)


def sent_together(arrays, axis, dim, along):
    ends, at = ([], 0)
    for a in arrays[:-1]:
        at += a.shape[along]
        ends.append(at)
    both = jnp.concatenate(arrays, axis=along)
    return tuple(jnp.split(lax.all_gather(both, axis, axis=dim, tiled=True), ends, axis=along))


def shortened(x):

    def short(part):
        return part.astype(jnp.bfloat16) if part.dtype == jnp.float32 else part

    return jax.tree.map(short, x)


def cut_along(x, dim, length):
    dims = x.shape
    pieces = x.reshape(*dims[:dim], length, dims[dim] // length, *dims[dim + 1 :])
    return jnp.moveaxis(pieces, dim, 0)


def sum_at_owner(x, axis, dim):
    length = lax.axis_size(axis)
    pieces = lax.all_to_all(cut_along(x, dim, length), axis, 0, 0, tiled=True)
    return jnp.sum(pieces.astype(jnp.float32), axis=0)


def tile_grads(tile_items):
    query_rows, grad_rows, key_rows, value_rows, trunk_keys_all, trunk_vals_all, length, parent = (
        tile_items
    )
    row_count = query_rows.shape[0]
    trunk_len = trunk_keys_all.shape[0]
    heads_kv = key_rows.shape[1] // HEAD_SIZE
    width_span = query_rows.shape[1] // heads_kv
    score_scale = 1.0 / math.sqrt(HEAD_SIZE)
    all_keys = jnp.concatenate([trunk_keys_all, key_rows], axis=0)
    all_values = jnp.concatenate([trunk_vals_all, value_rows], axis=0)
    row_ids = lax.broadcasted_iota(jnp.int32, (row_count, trunk_len + row_count), 0)
    col_ids = lax.broadcasted_iota(jnp.int32, (row_count, trunk_len + row_count), 1)
    allowed = jnp.where(col_ids < trunk_len, col_ids <= parent, col_ids - trunk_len <= row_ids)
    live_rows = (lax.broadcasted_iota(jnp.int32, (row_count, 1), 0) < length).astype(jnp.float32)
    query_parts, key_parts, value_parts = ([], [], [])
    for index_of_head in range(heads_kv):
        query_head = query_rows[
            :, index_of_head * width_span : (index_of_head + 1) * width_span
        ].reshape(row_count, width_span // HEAD_SIZE, HEAD_SIZE)
        grad_head = grad_rows[
            :, index_of_head * width_span : (index_of_head + 1) * width_span
        ].reshape(row_count, width_span // HEAD_SIZE, HEAD_SIZE)
        key_head = all_keys[:, index_of_head * HEAD_SIZE : (index_of_head + 1) * HEAD_SIZE]
        value_head = all_values[:, index_of_head * HEAD_SIZE : (index_of_head + 1) * HEAD_SIZE]
        scores = (
            jnp.einsum("igd,jd->gij", query_head, key_head, preferred_element_type=jnp.float32)
            * score_scale
        )
        scores = jnp.where(allowed[None], scores, masked_score)
        row_peak = jnp.max(scores, axis=-1, keepdims=True)
        exponent = jnp.where(allowed[None], jnp.exp(scores - row_peak), 0.0)
        weights = exponent / jnp.sum(exponent, axis=-1, keepdims=True) * live_rows[None]
        weights_low = weights.astype(jnp.bfloat16)
        grad_weights = jnp.einsum(
            "igd,jd->gij", grad_head, value_head, preferred_element_type=jnp.float32
        )
        row_delta = jnp.sum(weights * grad_weights, axis=-1, keepdims=True)
        dscore = (weights * (grad_weights - row_delta) * score_scale).astype(jnp.bfloat16)
        query_parts.append(
            jnp.einsum("gij,jd->igd", dscore, key_head, preferred_element_type=jnp.float32).reshape(
                row_count, width_span
            )
        )
        key_parts.append(
            jnp.einsum("gij,igd->jd", dscore, query_head, preferred_element_type=jnp.float32)
        )
        value_parts.append(
            jnp.einsum("gij,igd->jd", weights_low, grad_head, preferred_element_type=jnp.float32)
        )
    return (
        jnp.concatenate(query_parts, axis=1),
        jnp.concatenate(key_parts, axis=1),
        jnp.concatenate(value_parts, axis=1),
    )


def skipped(tile_items):
    row_count = tile_items[0].shape[0]
    total = tile_items[4].shape[0] + row_count
    return (
        jnp.zeros((row_count, tile_items[0].shape[1]), jnp.float32),
        jnp.zeros((total, tile_items[2].shape[1]), jnp.float32),
        jnp.zeros((total, tile_items[2].shape[1]), jnp.float32),
    )


def guarded(should_run, tile_items):
    return lax.cond(should_run, tile_grads, skipped, tile_items)


def per_device(
    queries,
    branch_key_rows,
    branch_value_rows,
    grad_output,
    trunk_keys,
    trunk_token_values,
    lengths,
    parents,
):
    query_full = queries[0]
    gradient_full = grad_output[0]
    key_full = branch_key_rows[0]
    value_full = branch_value_rows[0]
    own_trunk_keys = trunk_keys[0]
    own_trunk_vals = trunk_token_values[0]
    slot_count = lengths.shape[1]
    tile_rows = query_full.shape[0] // slot_count
    leaf_count = lax.axis_size("leaf")
    pair_bit = leaf_count.bit_length() - 2
    leaf_index = lax.axis_index("leaf")
    partner = jnp.bitwise_xor(leaf_index, leaf_count // 2)
    own_lengths = lax.dynamic_index_in_dim(lengths, leaf_index, 0, keepdims=False)
    own_parents = lax.dynamic_index_in_dim(parents, leaf_index, 0, keepdims=False)
    other_lengths = lax.dynamic_index_in_dim(lengths, partner, 0, keepdims=False)
    other_parents = lax.dynamic_index_in_dim(parents, partner, 0, keepdims=False)
    slot_ids = jnp.arange(slot_count, dtype=jnp.int32)
    own_count = jnp.sum((own_lengths > 0).astype(jnp.int32))
    other_count = jnp.sum((other_lengths > 0).astype(jnp.int32))
    lends = own_count - other_count >= 2
    helps = other_count - own_count >= 2
    own_pick = jnp.max(jnp.where(own_lengths > 0, slot_ids, 0))
    other_pick = jnp.max(jnp.where(other_lengths > 0, slot_ids, 0))

    def rows_of(source, pick):
        return lax.dynamic_slice_in_dim(source, pick * tile_rows, tile_rows, 0)

    got_query, got_grad, got_key, got_value = partner_2(
        (
            rows_of(query_full, own_pick),
            rows_of(gradient_full, own_pick),
            rows_of(key_full, own_pick),
            rows_of(value_full, own_pick),
        ),
        "leaf",
        pair_bit,
    )
    full_keys, full_vals = sent_together((own_trunk_keys, own_trunk_vals), "seq", 0, 1)
    other_keys, other_vals = partner_2((full_keys, full_vals), "leaf", pair_bit)
    trunk_len = full_keys.shape[0]

    def one_slot(partial_sums, slot_entries):
        query_rows, grad_rows, key_rows, value_rows, length, parent, slot_index = slot_entries
        should_run = (length > 0) & jnp.logical_not(lends & (slot_index == own_pick))
        results = guarded(
            should_run,
            (query_rows, grad_rows, key_rows, value_rows, full_keys, full_vals, length, parent),
        )
        new_sums = (
            partial_sums[0] + results[1][:trunk_len],
            partial_sums[1] + results[2][:trunk_len],
        )
        return (new_sums, (results[0], results[1][trunk_len:], results[2][trunk_len:]))

    initial_sums = (
        jnp.zeros((trunk_len, key_full.shape[1]), jnp.float32),
        jnp.zeros((trunk_len, key_full.shape[1]), jnp.float32),
    )
    slot_entries = (
        query_full.reshape(slot_count, tile_rows, -1),
        gradient_full.reshape(slot_count, tile_rows, -1),
        key_full.reshape(slot_count, tile_rows, -1),
        value_full.reshape(slot_count, tile_rows, -1),
        own_lengths,
        own_parents,
        slot_ids,
    )
    own_sums, tile_outputs = lax.scan(one_slot, initial_sums, slot_entries)
    grad_query_all = tile_outputs[0].reshape(slot_count * tile_rows, -1)
    grad_key_all = tile_outputs[1].reshape(slot_count * tile_rows, -1)
    grad_value_all = tile_outputs[2].reshape(slot_count * tile_rows, -1)
    help_length = lax.dynamic_index_in_dim(other_lengths, other_pick, 0, keepdims=False)
    help_parent = lax.dynamic_index_in_dim(other_parents, other_pick, 0, keepdims=False)
    help_query, help_key, help_value = guarded(
        helps,
        (got_query, got_grad, got_key, got_value, other_keys, other_vals, help_length, help_parent),
    )
    back_query, back_key, back_value = (
        partner_2(shortened(help_query), "leaf", pair_bit).astype(help_query.dtype),
        partner_2(shortened(help_key[trunk_len:]), "leaf", pair_bit),
        partner_2(shortened(help_value[trunk_len:]), "leaf", pair_bit),
    )

    def place(whole, returned):
        current = rows_of(whole, own_pick)
        return lax.dynamic_update_slice_in_dim(
            whole, jnp.where(lends, returned, current), own_pick * tile_rows, 0
        )

    grad_query_all = place(grad_query_all, back_query)
    grad_key_all = place(grad_key_all, back_key)
    grad_value_all = place(grad_value_all, back_value)
    trunk_key_grad, trunk_val_grad, help_key_share, help_val_share = (
        sum_at_owner(own_sums[0].astype(jnp.bfloat16), "seq", 0),
        sum_at_owner(own_sums[1].astype(jnp.bfloat16), "seq", 0),
        sum_at_owner(help_key[:trunk_len].astype(jnp.bfloat16), "seq", 0),
        sum_at_owner(help_value[:trunk_len].astype(jnp.bfloat16), "seq", 0),
    )
    back_key_share, back_val_share = partner_2((help_key_share, help_val_share), "leaf", pair_bit)
    trunk_key_grad = trunk_key_grad + back_key_share
    trunk_val_grad = trunk_val_grad + back_val_share
    return (
        grad_query_all[None],
        grad_key_all[None],
        grad_value_all[None],
        trunk_key_grad[None],
        trunk_val_grad[None],
    )


def solution(mesh):
    placed = (
        P("leaf", "seq", None),
        P("leaf", "seq", None),
        P("leaf", "seq", None),
        P("leaf", "seq", None),
        P("leaf", "seq", None),
        P("leaf", "seq", None),
        P(None, "seq"),
        P(None, "seq"),
    )
    return jax.shard_map(
        per_device,
        mesh=mesh,
        in_specs=placed,
        out_specs=(
            P("leaf", "seq", None),
            P("leaf", "seq", None),
            P("leaf", "seq", None),
            P("leaf", "seq", None),
            P("leaf", "seq", None),
        ),
        check_vma=False,
    )
```

profile of v0, /device:TPU:64, one launch (start us, length us, event | category | flops | bytes accessed | tf_op | source)
XLA Modules:
  0.0 552.9 jit_solution(3248955719673027018)
XLA Ops:
  1.3 84.7 %all_gather.3 = bf16[256,1024]{1,0:T(8,128)(2,1)S(1)} all-gather(bf16[8,1024]{1,0:T(8,128)(2,1)S(1)} %pad_maximum_fusion.7), channel_id=1, replica_groups=mesh['leaf'=8,'seq'=32] {'seq'}, dimensions={0}, use_global_device_ids=true | all-gather | bytes 540672 | tf_op jit(solution)/shard_map/all_gather | solution.py:30
  86.9 4.8 collective-permute-start.3
  96.9 4.8 collective-permute-start.2
  105.5 230.8 %while.19 = (s32[]{:T(128)}, f32[256,512]{1,0:T(8,128)}, f32[256,512]{1,0:T(8,128)}, f32[4,64,4096]{2,1,0:T(8,128)}, f32[4,64,512]{2,1,0:T(8,128)}, /*index=5*/f...) while((s32[]{:T(128)}, f32[256,512]{1,0:T(8,128)}, ...), condition=%wide.region_18.19_spmd.clone, body=%wide.region_3.18_spmd.clone.sunk | while | flops 860242752 | bytes 59644992 | solution.py:201
  108.5 66.0 %conditional.5 = (f32[1,64,4096]{2,1,0:T(8,128)S(1)}, f32[256,512]{1,0:T(8,128)S(1)}, f32[1,64,512]{2,1,0:T(8,128)}, f32[256,512]{1,0:T(8,128)S(1)}, f32[1,64,512]{2,1,0:T(8,128)}) conditional(s32[]{:T(128)} %convert_element_type.253, () %tuple.115, (bf16[4,64,512]{2,1,0:T(8,128)(2,1)}, s32[]{:T(128)}, bf16[256,512]{1,0:T(8,128)(2,1)}, ...), branch_computations={%region_4.4_spmd, %region_5.17_spmd} | conditional | flops 859718464 | bytes 53876484 | solution.py:121
  119.9 2.7 fusion.352
  124.2 4.2 convolution_bitcast_fusion.15
  128.5 4.6 convolution_bitcast_fusion.7
  138.6 4.9 convolution_bitcast_fusion.12
  143.5 4.6 convolution_bitcast_fusion.4
  152.8 4.2 convolution_bitcast_fusion.13
  157.0 3.9 convolution_bitcast_fusion.5
  163.2 3.9 convolution_bitcast_fusion.6
  167.0 4.2 convolution_bitcast_fusion.14
  182.9 2.4 select_add_fusion.3
  191.1 66.0 %conditional.5 = (f32[1,64,4096]{2,1,0:T(8,128)S(1)}, f32[256,512]{1,0:T(8,128)S(1)}, f32[1,64,512]{2,1,0:T(8,128)}, f32[256,512]{1,0:T(8,128)S(1)}, f32[1,64,512]{2,1,0:T(8,128)}) conditional(s32[]{:T(128)} %convert_element_type.253, () %tuple.115, (bf16[4,64,512]{2,1,0:T(8,128)(2,1)}, s32[]{:T(128)}, bf16[256,512]{1,0:T(8,128)(2,1)}, ...), branch_computations={%region_4.4_spmd, %region_5.17_spmd} | conditional | flops 859718464 | bytes 53876484 | solution.py:121
  202.5 2.7 fusion.352
  206.8 4.2 convolution_bitcast_fusion.15
  211.1 4.6 convolution_bitcast_fusion.7
  221.3 4.9 convolution_bitcast_fusion.12
  226.1 4.6 convolution_bitcast_fusion.4
  235.4 4.2 convolution_bitcast_fusion.13
  239.6 3.9 convolution_bitcast_fusion.5
  245.8 3.9 convolution_bitcast_fusion.6
  249.6 4.2 convolution_bitcast_fusion.14
  257.1 2.4 select_add_fusion.3
  265.2 66.0 %conditional.5 = (f32[1,64,4096]{2,1,0:T(8,128)S(1)}, f32[256,512]{1,0:T(8,128)S(1)}, f32[1,64,512]{2,1,0:T(8,128)}, f32[256,512]{1,0:T(8,128)S(1)}, f32[1,64,512]{2,1,0:T(8,128)}) conditional(s32[]{:T(128)} %convert_element_type.253, () %tuple.115, (bf16[4,64,512]{2,1,0:T(8,128)(2,1)}, s32[]{:T(128)}, bf16[256,512]{1,0:T(8,128)(2,1)}, ...), branch_computations={%region_4.4_spmd, %region_5.17_spmd} | conditional | flops 859718464 | bytes 53876484 | solution.py:121
  276.6 2.7 fusion.352
  280.9 4.2 convolution_bitcast_fusion.15
  285.2 4.6 convolution_bitcast_fusion.7
  295.3 4.9 convolution_bitcast_fusion.12
  300.2 4.6 convolution_bitcast_fusion.4
  309.5 4.2 convolution_bitcast_fusion.13
  313.7 3.9 convolution_bitcast_fusion.5
  319.9 3.9 convolution_bitcast_fusion.6
  323.7 4.2 convolution_bitcast_fusion.14
  338.1 4.1 all-to-all-start
  343.2 65.6 %collective-permute-start.5 = (bf16[64,4096]{1,0:T(8,128)(2,1)S(1)}, bf16[64,4096]{1,0:T(8,128)(2,1)S(1)}, u32[]{:S(2)}, u32[]{:S(2)}) collective-permute-start(bf16[64,4096]{1,0:T(8,128)(2,1)S(1)} %dynamic-slice_bitcast_fusion.4), channel_id=1, source_target_pairs={{0,128},{128,0},{32,160},{160,32},{64,192},{192,64},{96,224},{224,... | collective-permute-start | bytes 1572872 | tf_op jit(solution)/shard_map/ppermute | solution.py:21
  410.6 8.3 %all-to-all-start.2 = ((bf16[32,8,512]{2,1,0:T(8,128)(2,1)}), bf16[32,8,512]{2,1,0:T(8,128)(2,1)S(1)}, u32[]{:S(2)}, u32[]{:S(2)}) async-start(bf16[32,8,512]{2,1,0:T(8,128)(2,1)} %convert_bitcast_fusion), calls=%async_computation.2 | async-start | bytes 524288 | tf_op jit(solution)/shard_map/all_to_all | solution.py:49
  422.4 5.6 %collective-permute-done.1 = bf16[64,512]{1,0:T(8,128)(2,1)S(1)} collective-permute-done((bf16[64,512]{1,0:T(8,128)(2,1)S(1)}, bf16[64,512]{1,0:T(8,128)(2,1)S(1)}, u32[]{:S(2)}, u32[]{:S(2)}) %collective-permute-start.1) | collective-permute-done | bytes 65568 | tf_op jit(solution)/shard_map/ppermute | solution.py:21
  431.1 5.1 collective-permute-done.4
  437.8 75.6 %all-to-all-start.1 = ((bf16[32,8,512]{2,1,0:T(8,128)(2,1)}), bf16[32,8,512]{2,1,0:T(8,128)(2,1)S(1)}, u32[]{:S(2)}, u32[]{:S(2)}) async-start(bf16[32,8,512]{2,1,0:T(8,128)(2,1)} %slice_bitcast_fusion.53), calls=%async_computation.1 | async-start | bytes 524288 | tf_op jit(solution)/shard_map/all_to_all | solution.py:49
  513.5 4.7 copy.308
  519.9 5.9 %collective-permute-start.8 = (bf16[64,512]{1,0:T(8,128)(2,1)S(1)}, bf16[64,512]{1,0:T(8,128)(2,1)S(1)}, u32[]{:S(2)}, u32[]{:S(2)}) collective-permute-start(bf16[64,512]{1,0:T(8,128)(2,1)S(1)} %slice.281), channel_id=1, source_target_pairs={{0,128},{128,0},{32,160},{160,32},{64,192},{192,64},{96,224},{224,... | collective-permute-start | bytes 196616 | tf_op jit(solution)/shard_map/ppermute | solution.py:21
  525.9 8.3 %all-to-all-start.3 = ((bf16[32,8,512]{2,1,0:T(8,128)(2,1)}), bf16[32,8,512]{2,1,0:T(8,128)(2,1)S(1)}, u32[]{:S(2)}, u32[]{:S(2)}) async-start(bf16[32,8,512]{2,1,0:T(8,128)(2,1)} %slice_bitcast_fusion.52), calls=%async_computation.3 | async-start | bytes 524288 | tf_op jit(solution)/shard_map/all_to_all | solution.py:49
  534.4 5.9 %collective-permute-start.9 = (f32[8,512]{1,0:T(8,128)S(1)}, f32[8,512]{1,0:T(8,128)S(1)}, u32[]{:S(2)}, u32[]{:S(2)}) collective-permute-start(f32[8,512]{1,0:T(8,128)S(1)} %convert_reduce_fusion.2), channel_id=1, source_target_pairs={{0,128},{128,0},{32,160},{160,32},{64,192},{192,64},{96,224},{224,... | collective-permute-start | bytes 49160 | tf_op jit(solution)/shard_map/ppermute | solution.py:21
  540.3 3.1 all-to-all-done.3
  543.4 5.9 %collective-permute-start.10 = (f32[8,512]{1,0:T(8,128)S(1)}, f32[8,512]{1,0:T(8,128)S(1)}, u32[]{:S(2)}, u32[]{:S(2)}) collective-permute-start(f32[8,512]{1,0:T(8,128)S(1)} %convert_reduce_fusion), channel_id=1, source_target_pairs={{0,128},{128,0},{32,160},{160,32},{64,192},{192,64},{96,224},{224,... | collective-permute-start | bytes 49160 | tf_op jit(solution)/shard_map/ppermute | solution.py:21
  (282 shorter events, 134.1 us)
Async XLA Ops:
  86.9 349.2 %collective-permute-start.3 = (bf16[256,512]{1,0:T(8,128)(2,1)}, bf16[256,512]{1,0:T(8,128)(2,1)}, u32[]{:S(2)}, u32[]{:S(2)}) collective-permute-start(bf16[256,512]{1,0:T(8,128)(2,1)} %get-tuple-element.674), channel_id=1, source_target_pairs={{0,128},{128,0},{32,160},{160,32},{64,192},{192,64},{96,224},{224,... | collective-permute-start | bytes 786440 | tf_op jit(solution)/shard_map/ppermute | solution.py:21
  91.8 344.4 %collective-permute-start = (bf16[256,512]{1,0:T(8,128)(2,1)}, bf16[256,512]{1,0:T(8,128)(2,1)}, u32[]{:S(2)}, u32[]{:S(2)}) collective-permute-start(bf16[256,512]{1,0:T(8,128)(2,1)} %get-tuple-element.670), channel_id=1, source_target_pairs={{0,128},{128,0},{32,160},{160,32},{64,192},{192,64},{96,224},{224,... | collective-permute-start | bytes 786440 | tf_op jit(solution)/shard_map/ppermute | solution.py:21
  96.9 339.2 %collective-permute-start.2 = (bf16[64,4096]{1,0:T(8,128)(2,1)}, bf16[64,4096]{1,0:T(8,128)(2,1)}, u32[]{:S(2)}, u32[]{:S(2)}) collective-permute-start(bf16[64,4096]{1,0:T(8,128)(2,1)} %dynamic-slice_bitcast_fusion.5), channel_id=1, source_target_pairs={{0,128},{128,0},{32,160},{160,32},{64,192},{192,64},{96,224},{224,... | collective-permute-start | bytes 1572872 | tf_op jit(solution)/shard_map/ppermute | solution.py:21
  110.9 9.0 %copy-start.14 = (pred[64,320]{1,0:T(8,128)(4,1)}, pred[64,320]{1,0:T(8,128)(4,1)S(1)}, u32[]{:S(2)}) copy-start(pred[64,320]{1,0:T(8,128)(4,1)S(1)} %fusion.104) | copy-start | bytes 61444 | tf_op jit(solution)/shard_map/while/body/eval_jaxpr/cond
  115.4 7.3 %copy-start.10 = (bf16[8,8,8,128]{3,2,1,0:T(8,128)(2,1)}, bf16[8,8,8,128]{3,2,1,0:T(8,128)(2,1)S(1)}, u32[]{:S(2)}) copy-start(bf16[8,8,8,128]{3,2,1,0:T(8,128)(2,1)S(1)} %get-tuple-element.476) | copy-start | bytes 393220 | tf_op jit(solution)/shard_map/while/body/eval_jaxpr/cond
  136.4 7.2 %copy-start.11 = (bf16[320,128,1]{1,0,2:T(8,128)(2,1)S(1)}, bf16[320,128,1]{1,0,2:T(8,128)(2,1)}, u32[]{:S(2)}) copy-start(bf16[320,128,1]{1,0,2:T(8,128)(2,1)} %fusion.123) | copy-start | bytes 245764 | tf_op jit(solution)/shard_map/while/body/eval_jaxpr/cond
  138.6 10.4 %copy-start.8 = (bf16[8,8,8,128]{3,2,1,0:T(8,128)(2,1)S(1)}, bf16[8,8,8,128]{3,2,1,0:T(8,128)(2,1)}, u32[]{:S(2)}) copy-start(bf16[8,8,8,128]{3,2,1,0:T(8,128)(2,1)} %get-tuple-element.478) | copy-start | bytes 393220 | tf_op jit(solution)/shard_map/while/body/eval_jaxpr/cond
  143.5 7.7 %copy-start.5 = (bf16[8,8,8,128]{3,2,1,0:T(8,128)(2,1)S(1)}, bf16[8,8,8,128]{3,2,1,0:T(8,128)(2,1)}, u32[]{:S(2)}) copy-start(bf16[8,8,8,128]{3,2,1,0:T(8,128)(2,1)} %copy-done.4) | copy-start | bytes 393220 | tf_op jit(solution)/shard_map/while/body/eval_jaxpr/cond
  152.8 8.2 %copy-start.7 = (bf16[8,8,8,128]{3,2,1,0:T(8,128)(2,1)S(1)}, bf16[8,8,8,128]{3,2,1,0:T(8,128)(2,1)}, u32[]{:S(2)}) copy-start(bf16[8,8,8,128]{3,2,1,0:T(8,128)(2,1)} %get-tuple-element.479) | copy-start | bytes 393220 | tf_op jit(solution)/shard_map/while/body/eval_jaxpr/cond
  152.8 8.2 %copy-start.15 = (pred[64,320]{1,0:T(8,128)(4,1)S(1)}, pred[64,320]{1,0:T(8,128)(4,1)}, u32[]{:S(2)}) copy-start(pred[64,320]{1,0:T(8,128)(4,1)} %copy-done.14) | copy-start | bytes 61444 | tf_op jit(solution)/shard_map/while/body/eval_jaxpr/cond
  163.2 8.1 %copy-start.3 = (bf16[8,8,8,128]{3,2,1,0:T(8,128)(2,1)S(1)}, bf16[8,8,8,128]{3,2,1,0:T(8,128)(2,1)}, u32[]{:S(2)}) copy-start(bf16[8,8,8,128]{3,2,1,0:T(8,128)(2,1)} %copy-done.2) | copy-start | bytes 393220 | tf_op jit(solution)/shard_map/while/body/eval_jaxpr/cond
  167.0 5.9 %copy-start.1 = (f32[320,128]{1,0:T(8,128)S(1)}, f32[320,128]{1,0:T(8,128)}, u32[]{:S(2)}) copy-start(f32[320,128]{1,0:T(8,128)} %convolution_bitcast_fusion.8) | copy-start | bytes 491524 | tf_op jit(solution)/shard_map/while/body/eval_jaxpr/cond
  193.5 9.0 %copy-start.14 = (pred[64,320]{1,0:T(8,128)(4,1)}, pred[64,320]{1,0:T(8,128)(4,1)S(1)}, u32[]{:S(2)}) copy-start(pred[64,320]{1,0:T(8,128)(4,1)S(1)} %fusion.104) | copy-start | bytes 61444 | tf_op jit(solution)/shard_map/while/body/eval_jaxpr/cond
  198.1 7.2 %copy-start.10 = (bf16[8,8,8,128]{3,2,1,0:T(8,128)(2,1)}, bf16[8,8,8,128]{3,2,1,0:T(8,128)(2,1)S(1)}, u32[]{:S(2)}) copy-start(bf16[8,8,8,128]{3,2,1,0:T(8,128)(2,1)S(1)} %get-tuple-element.476) | copy-start | bytes 393220 | tf_op jit(solution)/shard_map/while/body/eval_jaxpr/cond
  215.7 5.6 %copy-start.25 = (f32[64]{0:T(128)S(1)}, f32[64]{0:T(128)}, u32[]{:S(2)}) copy-start(f32[64]{0:T(128)} %compare_convert_fusion) | copy-start | bytes 772 | tf_op jit(solution)/shard_map/while/body/eval_jaxpr/cond
  219.0 7.2 %copy-start.11 = (bf16[320,128,1]{1,0,2:T(8,128)(2,1)S(1)}, bf16[320,128,1]{1,0,2:T(8,128)(2,1)}, u32[]{:S(2)}) copy-start(bf16[320,128,1]{1,0,2:T(8,128)(2,1)} %fusion.123) | copy-start | bytes 245764 | tf_op jit(solution)/shard_map/while/body/eval_jaxpr/cond
  221.2 10.4 %copy-start.8 = (bf16[8,8,8,128]{3,2,1,0:T(8,128)(2,1)S(1)}, bf16[8,8,8,128]{3,2,1,0:T(8,128)(2,1)}, u32[]{:S(2)}) copy-start(bf16[8,8,8,128]{3,2,1,0:T(8,128)(2,1)} %get-tuple-element.478) | copy-start | bytes 393220 | tf_op jit(solution)/shard_map/while/body/eval_jaxpr/cond
  226.1 7.7 %copy-start.5 = (bf16[8,8,8,128]{3,2,1,0:T(8,128)(2,1)S(1)}, bf16[8,8,8,128]{3,2,1,0:T(8,128)(2,1)}, u32[]{:S(2)}) copy-start(bf16[8,8,8,128]{3,2,1,0:T(8,128)(2,1)} %copy-done.4) | copy-start | bytes 393220 | tf_op jit(solution)/shard_map/while/body/eval_jaxpr/cond
  235.4 8.2 %copy-start.7 = (bf16[8,8,8,128]{3,2,1,0:T(8,128)(2,1)S(1)}, bf16[8,8,8,128]{3,2,1,0:T(8,128)(2,1)}, u32[]{:S(2)}) copy-start(bf16[8,8,8,128]{3,2,1,0:T(8,128)(2,1)} %get-tuple-element.479) | copy-start | bytes 393220 | tf_op jit(solution)/shard_map/while/body/eval_jaxpr/cond
  235.4 8.2 %copy-start.15 = (pred[64,320]{1,0:T(8,128)(4,1)S(1)}, pred[64,320]{1,0:T(8,128)(4,1)}, u32[]{:S(2)}) copy-start(pred[64,320]{1,0:T(8,128)(4,1)} %copy-done.14) | copy-start | bytes 61444 | tf_op jit(solution)/shard_map/while/body/eval_jaxpr/cond
  245.8 8.1 %copy-start.3 = (bf16[8,8,8,128]{3,2,1,0:T(8,128)(2,1)S(1)}, bf16[8,8,8,128]{3,2,1,0:T(8,128)(2,1)}, u32[]{:S(2)}) copy-start(bf16[8,8,8,128]{3,2,1,0:T(8,128)(2,1)} %copy-done.2) | copy-start | bytes 393220 | tf_op jit(solution)/shard_map/while/body/eval_jaxpr/cond
  249.6 5.9 %copy-start.1 = (f32[320,128]{1,0:T(8,128)S(1)}, f32[320,128]{1,0:T(8,128)}, u32[]{:S(2)}) copy-start(f32[320,128]{1,0:T(8,128)} %convolution_bitcast_fusion.8) | copy-start | bytes 491524 | tf_op jit(solution)/shard_map/while/body/eval_jaxpr/cond
  267.6 9.0 %copy-start.14 = (pred[64,320]{1,0:T(8,128)(4,1)}, pred[64,320]{1,0:T(8,128)(4,1)S(1)}, u32[]{:S(2)}) copy-start(pred[64,320]{1,0:T(8,128)(4,1)S(1)} %fusion.104) | copy-start | bytes 61444 | tf_op jit(solution)/shard_map/while/body/eval_jaxpr/cond
  272.1 7.2 %copy-start.10 = (bf16[8,8,8,128]{3,2,1,0:T(8,128)(2,1)}, bf16[8,8,8,128]{3,2,1,0:T(8,128)(2,1)S(1)}, u32[]{:S(2)}) copy-start(bf16[8,8,8,128]{3,2,1,0:T(8,128)(2,1)S(1)} %get-tuple-element.476) | copy-start | bytes 393220 | tf_op jit(solution)/shard_map/while/body/eval_jaxpr/cond
  293.1 7.2 %copy-start.11 = (bf16[320,128,1]{1,0,2:T(8,128)(2,1)S(1)}, bf16[320,128,1]{1,0,2:T(8,128)(2,1)}, u32[]{:S(2)}) copy-start(bf16[320,128,1]{1,0,2:T(8,128)(2,1)} %fusion.123) | copy-start | bytes 245764 | tf_op jit(solution)/shard_map/while/body/eval_jaxpr/cond
  295.3 10.4 %copy-start.8 = (bf16[8,8,8,128]{3,2,1,0:T(8,128)(2,1)S(1)}, bf16[8,8,8,128]{3,2,1,0:T(8,128)(2,1)}, u32[]{:S(2)}) copy-start(bf16[8,8,8,128]{3,2,1,0:T(8,128)(2,1)} %get-tuple-element.478) | copy-start | bytes 393220 | tf_op jit(solution)/shard_map/while/body/eval_jaxpr/cond
  300.2 7.7 %copy-start.5 = (bf16[8,8,8,128]{3,2,1,0:T(8,128)(2,1)S(1)}, bf16[8,8,8,128]{3,2,1,0:T(8,128)(2,1)}, u32[]{:S(2)}) copy-start(bf16[8,8,8,128]{3,2,1,0:T(8,128)(2,1)} %copy-done.4) | copy-start | bytes 393220 | tf_op jit(solution)/shard_map/while/body/eval_jaxpr/cond
  309.5 8.2 %copy-start.7 = (bf16[8,8,8,128]{3,2,1,0:T(8,128)(2,1)S(1)}, bf16[8,8,8,128]{3,2,1,0:T(8,128)(2,1)}, u32[]{:S(2)}) copy-start(bf16[8,8,8,128]{3,2,1,0:T(8,128)(2,1)} %get-tuple-element.479) | copy-start | bytes 393220 | tf_op jit(solution)/shard_map/while/body/eval_jaxpr/cond
  309.5 8.2 %copy-start.15 = (pred[64,320]{1,0:T(8,128)(4,1)S(1)}, pred[64,320]{1,0:T(8,128)(4,1)}, u32[]{:S(2)}) copy-start(pred[64,320]{1,0:T(8,128)(4,1)} %copy-done.14) | copy-start | bytes 61444 | tf_op jit(solution)/shard_map/while/body/eval_jaxpr/cond
  319.9 8.1 %copy-start.3 = (bf16[8,8,8,128]{3,2,1,0:T(8,128)(2,1)S(1)}, bf16[8,8,8,128]{3,2,1,0:T(8,128)(2,1)}, u32[]{:S(2)}) copy-start(bf16[8,8,8,128]{3,2,1,0:T(8,128)(2,1)} %copy-done.2) | copy-start | bytes 393220 | tf_op jit(solution)/shard_map/while/body/eval_jaxpr/cond
  323.7 5.9 %copy-start.1 = (f32[320,128]{1,0:T(8,128)S(1)}, f32[320,128]{1,0:T(8,128)}, u32[]{:S(2)}) copy-start(f32[320,128]{1,0:T(8,128)} %convolution_bitcast_fusion.8) | copy-start | bytes 491524 | tf_op jit(solution)/shard_map/while/body/eval_jaxpr/cond
  338.1 72.6 %all-to-all-start = ((bf16[32,8,512]{2,1,0:T(8,128)(2,1)}), bf16[32,8,512]{2,1,0:T(8,128)(2,1)S(1)}, u32[]{:S(2)}, u32[]{:S(2)}) async-start(bf16[32,8,512]{2,1,0:T(8,128)(2,1)} %convert_bitcast_fusion.1), calls=%async_computation | async-start | bytes 524288 | tf_op jit(solution)/shard_map/all_to_all | solution.py:49
  343.2 92.9 %collective-permute-start.5 = (bf16[64,4096]{1,0:T(8,128)(2,1)S(1)}, bf16[64,4096]{1,0:T(8,128)(2,1)S(1)}, u32[]{:S(2)}, u32[]{:S(2)}) collective-permute-start(bf16[64,4096]{1,0:T(8,128)(2,1)S(1)} %dynamic-slice_bitcast_fusion.4), channel_id=1, source_target_pairs={{0,128},{128,0},{32,160},{160,32},{64,192},{192,64},{96,224},{224,... | collective-permute-start | bytes 1572872 | tf_op jit(solution)/shard_map/ppermute | solution.py:21
  410.6 27.2 %all-to-all-start.2 = ((bf16[32,8,512]{2,1,0:T(8,128)(2,1)}), bf16[32,8,512]{2,1,0:T(8,128)(2,1)S(1)}, u32[]{:S(2)}, u32[]{:S(2)}) async-start(bf16[32,8,512]{2,1,0:T(8,128)(2,1)} %convert_bitcast_fusion), calls=%async_computation.2 | async-start | bytes 524288 | tf_op jit(solution)/shard_map/all_to_all | solution.py:49
  419.8 8.2 %collective-permute-start.1 = (bf16[64,512]{1,0:T(8,128)(2,1)S(1)}, bf16[64,512]{1,0:T(8,128)(2,1)S(1)}, u32[]{:S(2)}, u32[]{:S(2)}) collective-permute-start(bf16[64,512]{1,0:T(8,128)(2,1)S(1)} %dynamic-slice_bitcast_fusion.7), channel_id=1, source_target_pairs={{0,128},{128,0},{32,160},{160,32},{64,192},{192,64},{96,224},{224,... | collective-permute-start | bytes 196616 | tf_op jit(solution)/shard_map/ppermute | solution.py:21
  428.0 8.2 %collective-permute-start.4 = (bf16[64,512]{1,0:T(8,128)(2,1)S(1)}, bf16[64,512]{1,0:T(8,128)(2,1)S(1)}, u32[]{:S(2)}, u32[]{:S(2)}) collective-permute-start(bf16[64,512]{1,0:T(8,128)(2,1)S(1)} %dynamic-slice_bitcast_fusion.6), channel_id=1, source_target_pairs={{0,128},{128,0},{32,160},{160,32},{64,192},{192,64},{96,224},{224,... | collective-permute-start | bytes 196616 | tf_op jit(solution)/shard_map/ppermute | solution.py:21
  436.2 77.2 %copy-start.13 = (f32[4,64,512]{2,1,0:T(8,128)S(1)}, f32[4,64,512]{2,1,0:T(8,128)}, u32[]{:S(2)}) copy-start(f32[4,64,512]{2,1,0:T(8,128)} %get-tuple-element.375) | copy-start | bytes 1572868
  436.2 77.3 %copy-start.12 = (f32[4,64,512]{2,1,0:T(8,128)S(1)}, f32[4,64,512]{2,1,0:T(8,128)}, u32[]{:S(2)}) copy-start(f32[4,64,512]{2,1,0:T(8,128)} %get-tuple-element.377) | copy-start | bytes 1572868
  437.8 88.1 %all-to-all-start.1 = ((bf16[32,8,512]{2,1,0:T(8,128)(2,1)}), bf16[32,8,512]{2,1,0:T(8,128)(2,1)S(1)}, u32[]{:S(2)}, u32[]{:S(2)}) async-start(bf16[32,8,512]{2,1,0:T(8,128)(2,1)} %slice_bitcast_fusion.53), calls=%async_computation.1 | async-start | bytes 524288 | tf_op jit(solution)/shard_map/all_to_all | solution.py:49
  518.8 32.8 %copy-start.24 = (f32[8,512]{1,0:T(8,128)S(1)}, f32[8,512]{1,0:T(8,128)}, u32[]{:S(2)}) copy-start(f32[8,512]{1,0:T(8,128)} %convert_reduce_fusion.3) | copy-start | bytes 49156
  518.9 15.4 %collective-permute-start.7 = (bf16[64,512]{1,0:T(8,128)(2,1)S(1)}, bf16[64,512]{1,0:T(8,128)(2,1)S(1)}, u32[]{:S(2)}, u32[]{:S(2)}) collective-permute-start(bf16[64,512]{1,0:T(8,128)(2,1)S(1)} %slice.280), channel_id=1, source_target_pairs={{0,128},{128,0},{32,160},{160,32},{64,192},{192,64},{96,224},{224,... | collective-permute-start | bytes 196616 | tf_op jit(solution)/shard_map/ppermute | solution.py:21
  519.9 14.4 %collective-permute-start.8 = (bf16[64,512]{1,0:T(8,128)(2,1)S(1)}, bf16[64,512]{1,0:T(8,128)(2,1)S(1)}, u32[]{:S(2)}, u32[]{:S(2)}) collective-permute-start(bf16[64,512]{1,0:T(8,128)(2,1)S(1)} %slice.281), channel_id=1, source_target_pairs={{0,128},{128,0},{32,160},{160,32},{64,192},{192,64},{96,224},{224,... | collective-permute-start | bytes 196616 | tf_op jit(solution)/shard_map/ppermute | solution.py:21
  525.8 23.5 %collective-permute-start.6 = (bf16[64,4096]{1,0:T(8,128)(2,1)}, bf16[64,4096]{1,0:T(8,128)(2,1)S(1)}, u32[]{:S(2)}, u32[]{:S(2)}) collective-permute-start(bf16[64,4096]{1,0:T(8,128)(2,1)} %get-tuple-element.374), channel_id=1, source_target_pairs={{0,128},{128,0},{32,160},{160,32},{64,192},{192,64},{96,224},{224,... | collective-permute-start | bytes 1572872 | tf_op jit(solution)/shard_map/ppermute | solution.py:21
  525.9 17.4 %all-to-all-start.3 = ((bf16[32,8,512]{2,1,0:T(8,128)(2,1)}), bf16[32,8,512]{2,1,0:T(8,128)(2,1)S(1)}, u32[]{:S(2)}, u32[]{:S(2)}) async-start(bf16[32,8,512]{2,1,0:T(8,128)(2,1)} %slice_bitcast_fusion.52), calls=%async_computation.3 | async-start | bytes 524288 | tf_op jit(solution)/shard_map/all_to_all | solution.py:49
  534.3 18.6 %copy-start.17 = (f32[1,256,512]{2,1,0:T(8,128)}, f32[1,256,512]{2,1,0:T(8,128)S(1)}, u32[]{:S(2)}) copy-start(f32[1,256,512]{2,1,0:T(8,128)S(1)} %bitcast_dynamic-update-slice_fusion.2) | copy-start | bytes 1572868
  534.3 18.6 %copy-start.16 = (f32[1,256,512]{2,1,0:T(8,128)}, f32[1,256,512]{2,1,0:T(8,128)S(1)}, u32[]{:S(2)}) copy-start(f32[1,256,512]{2,1,0:T(8,128)S(1)} %bitcast_dynamic-update-slice_fusion.1) | copy-start | bytes 1572868
  534.4 17.3 %collective-permute-start.9 = (f32[8,512]{1,0:T(8,128)S(1)}, f32[8,512]{1,0:T(8,128)S(1)}, u32[]{:S(2)}, u32[]{:S(2)}) collective-permute-start(f32[8,512]{1,0:T(8,128)S(1)} %convert_reduce_fusion.2), channel_id=1, source_target_pairs={{0,128},{128,0},{32,160},{160,32},{64,192},{192,64},{96,224},{224,... | collective-permute-start | bytes 49160 | tf_op jit(solution)/shard_map/ppermute | solution.py:21
  543.4 8.8 %collective-permute-start.10 = (f32[8,512]{1,0:T(8,128)S(1)}, f32[8,512]{1,0:T(8,128)S(1)}, u32[]{:S(2)}, u32[]{:S(2)}) collective-permute-start(f32[8,512]{1,0:T(8,128)S(1)} %convert_reduce_fusion), channel_id=1, source_target_pairs={{0,128},{128,0},{32,160},{160,32},{64,192},{192,64},{96,224},{224,... | collective-permute-start | bytes 49160 | tf_op jit(solution)/shard_map/ppermute | solution.py:21
  (20 other events, 77.2 us)
where the time goes:
time: 553 us
  starting transfers between devices  194 us (35%)
  matrix products  165 us (30%)
  blocking collectives  84.7 us (15%)
  local copies, waits for them, and re-layouts  48.8 us (9%)
  other arithmetic  33.5 us (6%)
  waiting for transfers between devices  13.7 us (2%)
  loops' own time  8.35 us (2%)
    ppermute x11, starting transfers between devices, partner_2(): return lax.ppermute(block, axis, route)  98.1 us
    all_to_all x4, starting transfers between devices, sum_at_owner(): pieces = lax.all_to_all(cut_along(x, dim, length), axis, 0, 0, tiled=True)  96.2 us
    all_gather x1, blocking collectives, sent_together(): lax.all_gather(both, axis, axis=dim, tiled=True)  84.7 us
    dot_general x12, matrix products, tile_grads(): jnp.einsum('gij,igd->jd', dscore, query_head, preferred_element_type=jnp....  52.5 us
    dot_general x12, matrix products, tile_grads(): jnp.einsum('gij,jd->igd', dscore, key_head, preferred_element_type=jnp.fl...  50.8 us
    sub x12, matrix products, tile_grads(): exponent = jnp.where(allowed[None], jnp.exp(scores - row_peak), 0.0)  28.1 us
    dot_general x12, matrix products, tile_grads(): jnp.einsum('gij,igd->jd', weights_low, grad_head, preferred_element_type=...  20.8 us
    dot_general x12, matrix products, tile_grads(): jnp.einsum('igd,jd->gij', grad_head, value_head, preferred_element_type=j...  13.3 us
  transfers between devices with their start and end apart: 15, of which 3 were waited for; matrix products, arithmetic and copies ran while one was open for 44% of the time, Pallas kernels for 0%

commit v1 on v0

v1 whole, which is shorter than its diff:
```python
import math

import jax
import jax.numpy as jnp
from jax import lax
from jax.experimental import pallas as pl
from jax.experimental.pallas import tpu as pltpu
from jax.sharding import PartitionSpec as P

HEAD_SIZE = 128
MASKED = -1e30
CHUNK = 256


def dot_nt(a, b):
    return lax.dot_general(a, b, (((1,), (1,)), ((), ())), preferred_element_type=jnp.float32)


def dot_tn(a, b):
    return lax.dot_general(a, b, (((0,), (0,)), ((), ())), preferred_element_type=jnp.float32)


def dot_nn(a, b):
    return lax.dot_general(a, b, (((1,), (0,)), ((), ())), preferred_element_type=jnp.float32)


def lanes(start):
    if isinstance(start, int):
        return slice(start, start + HEAD_SIZE)
    return pl.ds(pl.multiple_of(start, HEAD_SIZE), HEAD_SIZE)


def iota(shape, dim):
    return lax.broadcasted_iota(jnp.int32, shape, dim)


def score_kernel(
    leaf,
    lengths,
    parents,
    q_hbm,
    do_hbm,
    kv,
    kb_hbm,
    vb_hbm,
    sums,
    ds_hbm,
    pb_hbm,
    kv_hbm,
    q,
    do,
    kb,
    vb,
    ds_buf,
    pb_buf,
    key_mask,
    sems_in,
    sems_out,
    *,
    tiles,
):
    rows = q_hbm.shape[0] // tiles
    trunk = kv.shape[0]
    width = kb.shape[1]
    heads = width // HEAD_SIZE
    group_width = q_hbm.shape[1] // heads

    def fetches(h):
        span = pl.ds(pl.multiple_of(h * group_width, group_width), group_width)
        return [
            pltpu.make_async_copy(q_hbm.at[:, span], q.at[h], sems_in.at[0, h]),
            pltpu.make_async_copy(do_hbm.at[:, span], do.at[h], sems_in.at[1, h]),
        ]

    def stores(h):
        return [
            pltpu.make_async_copy(ds_buf.at[:, h], ds_hbm.at[:, h], sems_out.at[0, h]),
            pltpu.make_async_copy(pb_buf.at[:, h], pb_hbm.at[:, h], sems_out.at[1, h]),
        ]

    branch_fetches = [
        pltpu.make_async_copy(kb_hbm, kb, sems_in.at[0, heads]),
        pltpu.make_async_copy(vb_hbm, vb, sems_in.at[1, heads]),
    ]
    kv_store = pltpu.make_async_copy(kv, kv_hbm, sems_out.at[0, heads])
    for copy in fetches(0) + branch_fetches:
        copy.start()
    for h in range(1, heads):
        for copy in fetches(h):
            copy.start()
    kv_store.start()
    per_chunk = CHUNK // rows
    chunk_width = per_chunk * HEAD_SIZE
    halves = group_width // chunk_width
    scale = 1.0 / math.sqrt(HEAD_SIZE)
    to_exp2 = scale * math.log2(math.e)
    tree = leaf[0]

    shape = (CHUNK, HEAD_SIZE)
    column, row = iota(shape, 1), jnp.bitwise_and(iota(shape, 0), rows - 1)
    query_mask = jnp.where(
        column < rows,
        jnp.where(column > row, MASKED, 0.0),
        jnp.where(column == rows, 1.0, 0.0),
    ).astype(jnp.bfloat16)
    shape = (trunk + rows, HEAD_SIZE)
    column, row = iota(shape, 1), iota(shape, 0)
    branch_part = jnp.where(row == column + trunk, 1.0, 0.0)
    for t in range(tiles):
        key_mask[t] = jnp.where(
            (column == rows) & (row > parents[tree, t]) & (row < trunk),
            MASKED,
            jnp.where(column < rows, branch_part, 0.0),
        ).astype(jnp.bfloat16)
    lane_row = jnp.bitwise_and(iota((1, CHUNK), 1), rows - 1)
    live = [jnp.where(lane_row < lengths[tree, t], 1.0, 0.0) for t in range(tiles)]

    for copy in branch_fetches:
        copy.wait()

    def head_step(h, carry):
        for copy in fetches(h):
            copy.wait()

        def stacked(ref, t, half):
            first = half * chunk_width
            return jnp.concatenate(
                [
                    ref[h, t * rows : (t + 1) * rows, lanes(first + j * HEAD_SIZE)]
                    for j in range(per_chunk)
                ],
                axis=0,
            )

        trunk_keys = kv[:, lanes(h * HEAD_SIZE)]
        trunk_vals = kv[:, lanes(width + h * HEAD_SIZE)]

        def matmuls(c):
            t, half = c // halves, c % halves
            tile = slice(t * rows, (t + 1) * rows)
            queries, grads = stacked(q, t, half), stacked(do, t, half)
            keys = jnp.concatenate([trunk_keys, kb[tile, lanes(h * HEAD_SIZE)]], axis=0)
            values = jnp.concatenate([trunk_vals, vb[tile, lanes(h * HEAD_SIZE)]], axis=0)
            scores = dot_nt(
                jnp.concatenate([keys, key_mask[t]], axis=1),
                jnp.concatenate([queries, query_mask], axis=1),
            )
            return scores, dot_nt(values, grads), queries, grads

        def softmax(c, scores, grad_weights):
            t, half = c // halves, c % halves
            peak = jnp.max(scores, axis=0, keepdims=True)
            e = jnp.exp2((scores - peak) * to_exp2)
            inv = live[t] / jnp.sum(e, axis=0, keepdims=True)
            delta = inv * jnp.sum(e * grad_weights, axis=0, keepdims=True)
            weights = e * inv
            low = weights.astype(jnp.bfloat16)
            ds = (weights * (grad_weights - delta)).astype(jnp.bfloat16)
            part = slice(half * CHUNK, (half + 1) * CHUNK)
            ds_buf[t, h, :, part] = ds
            pb_buf[t, h, :, part] = low[trunk:]
            return ds[:trunk], low[:trunk]

        chunks = tiles * halves
        key_sum = value_sum = None
        ahead = matmuls(0)
        for c in range(chunks):
            scores, grad_weights, queries, grads = ahead
            if c + 1 < chunks:
                ahead = matmuls(c + 1)
            ds, low = softmax(c, scores, grad_weights)
            key_part, value_part = dot_nn(ds, queries), dot_nn(low, grads)
            key_sum = key_part if c == 0 else key_sum + key_part
            value_sum = value_part if c == 0 else value_sum + value_part
        shape = (sums.shape[0], sums.shape[2], HEAD_SIZE)
        sums[:, 0, :, lanes(h * HEAD_SIZE)] = (
            (key_sum * scale).reshape(shape).astype(jnp.bfloat16)
        )
        sums[:, 1, :, lanes(h * HEAD_SIZE)] = value_sum.reshape(shape).astype(jnp.bfloat16)
        for copy in stores(h):
            copy.start()
        return carry

    lax.fori_loop(0, heads, head_step, 0)
    kv_store.wait()
    for h in range(heads):
        for copy in stores(h):
            copy.wait()


def grad_kernel(
    q_hbm,
    do_hbm,
    kv,
    kb_hbm,
    ds_hbm,
    pb_hbm,
    dq,
    dkb,
    dvb,
    q,
    do,
    kb,
    ds,
    pb,
    dq_buf,
    dkb_buf,
    dvb_buf,
    sems_in,
    sems,
    *,
    tiles,
):
    rows = q_hbm.shape[0] // tiles
    trunk = kv.shape[0]
    heads = kb.shape[1] // HEAD_SIZE
    group_width = q.shape[1] // heads
    groups = group_width // HEAD_SIZE
    scale = 1.0 / math.sqrt(HEAD_SIZE)

    def fetches(t):
        tile = pl.ds(pl.multiple_of(t * rows, rows), rows)
        return [
            pltpu.make_async_copy(source.at[part], buf.at[part], sems_in.at[i, t])
            for i, (source, buf, part) in enumerate(
                (
                    (ds_hbm, ds, t),
                    (q_hbm, q, tile),
                    (do_hbm, do, tile),
                    (pb_hbm, pb, t),
                    (kb_hbm, kb, tile),
                )
            )
        ]

    for t in range(tiles):
        for copy in fetches(t):
            copy.start()

    def copies(t):
        tile = pl.ds(pl.multiple_of(t * rows, rows), rows)
        return [
            pltpu.make_async_copy(buf.at[tile], out.at[tile], sems.at[i, t])
            for i, (buf, out) in enumerate(((dq_buf, dq), (dkb_buf, dkb), (dvb_buf, dvb)))
        ]

    def tile_step(t, carry):
        for copy in fetches(t):
            copy.wait()
        tile = pl.ds(pl.multiple_of(t * rows, rows), rows)

        def stacked(ref, h):
            return jnp.concatenate(
                [ref[tile, lanes(h * group_width + j * HEAD_SIZE)] for j in range(groups)], axis=0
            )

        for h in range(heads):
            span = lanes(h * HEAD_SIZE)
            keys = jnp.concatenate([kv[:, span], kb[tile, span]], axis=0)
            dkb_buf[tile, span] = dot_nn(ds[t, h, trunk:, :], stacked(q, h)) * scale
            dvb_buf[tile, span] = dot_nn(pb[t, h], stacked(do, h))
            got = (dot_tn(keys, ds[t, h]) * scale).T
            for j in range(groups):
                dq_buf[tile, lanes(h * group_width + j * HEAD_SIZE)] = got[
                    j * rows : (j + 1) * rows
                ]
        for copy in copies(t):
            copy.start()
        return carry

    lax.fori_loop(0, tiles, tile_step, 0)
    for t in range(tiles):
        for copy in copies(t):
            copy.wait()


def per_device(
    queries,
    branch_key_rows,
    branch_value_rows,
    grad_output,
    trunk_keys,
    trunk_token_values,
    lengths,
    parents,
):
    q = queries[0]
    do = grad_output[0]
    kb = branch_key_rows[0]
    vb = branch_value_rows[0]
    seq = lax.axis_size("seq")
    leaf = lax.axis_index("leaf").astype(jnp.int32).reshape(1)
    tiles = lengths.shape[1]
    rows = q.shape[0] // tiles
    width = kb.shape[1]
    heads = width // HEAD_SIZE
    wide = q.shape[1] // width * rows
    own = trunk_keys.shape[1]
    trunk = own * seq
    work = heads * tiles * wide * (trunk + rows) * HEAD_SIZE * 2

    both = jnp.concatenate([trunk_keys[0], trunk_token_values[0]], axis=1)
    spread = jnp.broadcast_to(both[None], (seq,) + both.shape)
    gathered = lax.all_to_all(spread, "seq", 0, 0, tiled=True).reshape(trunk, 2 * width)

    vmem = pl.BlockSpec(memory_space=pltpu.VMEM)
    smem = pl.BlockSpec(memory_space=pltpu.SMEM)
    hbm = pl.BlockSpec(memory_space=pltpu.HBM)
    ds_shape = (tiles, heads, trunk + rows, wide)
    pb_shape = (tiles, heads, rows, wide)
    head_shape = (heads, tiles * rows, q.shape[1] // heads)

    sums, ds, pb, kv = pl.pallas_call(
        lambda *refs: score_kernel(*refs, tiles=tiles),
        in_specs=[smem] * 3 + [hbm, hbm, vmem, hbm, hbm],
        out_specs=[vmem, hbm, hbm, hbm],
        out_shape=[
            jax.ShapeDtypeStruct((seq, 2, own, width), jnp.bfloat16),
            jax.ShapeDtypeStruct(ds_shape, jnp.bfloat16),
            jax.ShapeDtypeStruct(pb_shape, jnp.bfloat16),
            jax.ShapeDtypeStruct(gathered.shape, jnp.bfloat16),
        ],
        scratch_shapes=[
            pltpu.VMEM(head_shape, jnp.bfloat16),
            pltpu.VMEM(head_shape, jnp.bfloat16),
            pltpu.VMEM(kb.shape, jnp.bfloat16),
            pltpu.VMEM(vb.shape, jnp.bfloat16),
            pltpu.VMEM(ds_shape, jnp.bfloat16),
            pltpu.VMEM(pb_shape, jnp.bfloat16),
            pltpu.VMEM((tiles, trunk + rows, HEAD_SIZE), jnp.bfloat16),
            pltpu.SemaphoreType.DMA((2, heads + 1)),
            pltpu.SemaphoreType.DMA((2, heads + 1)),
        ],
        compiler_params=pltpu.CompilerParams(vmem_limit_bytes=65_900_000),
        cost_estimate=pl.CostEstimate(
            flops=4 * work, bytes_accessed=12 << 20, transcendentals=work // 256
        ),
        name="scores",
    )(leaf, lengths, parents, q, do, gathered, kb, vb)

    shares = lax.all_to_all(sums, "seq", 0, 0, tiled=True)

    dq, dkb, dvb = pl.pallas_call(
        lambda *refs: grad_kernel(*refs, tiles=tiles),
        in_specs=[hbm, hbm, vmem, hbm, hbm, hbm],
        out_specs=[hbm] * 3,
        out_shape=[
            jax.ShapeDtypeStruct(q.shape, jnp.float32),
            jax.ShapeDtypeStruct(kb.shape, jnp.float32),
            jax.ShapeDtypeStruct(vb.shape, jnp.float32),
        ],
        scratch_shapes=[
            pltpu.VMEM(q.shape, jnp.bfloat16),
            pltpu.VMEM(q.shape, jnp.bfloat16),
            pltpu.VMEM(kb.shape, jnp.bfloat16),
            pltpu.VMEM(ds_shape, jnp.bfloat16),
            pltpu.VMEM(pb_shape, jnp.bfloat16),
            pltpu.VMEM(q.shape, jnp.float32),
            pltpu.VMEM(kb.shape, jnp.float32),
            pltpu.VMEM(vb.shape, jnp.float32),
            pltpu.SemaphoreType.DMA((5, tiles)),
            pltpu.SemaphoreType.DMA((3, tiles)),
        ],
        compiler_params=pltpu.CompilerParams(vmem_limit_bytes=65_900_000),
        cost_estimate=pl.CostEstimate(flops=2 * work, bytes_accessed=16 << 20, transcendentals=0),
        name="grads",
    )(q, do, kv, kb, ds, pb)

    trunk_grads = jnp.sum(shares.astype(jnp.float32), axis=0)
    return dq[None], dkb[None], dvb[None], trunk_grads[0][None], trunk_grads[1][None]


def solution(mesh):
    split = P("leaf", "seq", None)
    return jax.shard_map(
        per_device,
        mesh=mesh,
        in_specs=(split,) * 6 + (P(None, "seq"),) * 2,
        out_specs=(split,) * 5,
        check_vma=False,
    )
```

time: 553 us -> 53 us (0.10)
  starting transfers between devices: 194 us -> 12.7 us
  matrix products: 165 us -> 0 us
  blocking collectives: 84.7 us -> 0 us
  local copies, waits for them, and re-layouts: 48.8 us -> 4.96 us
  other arithmetic: 33.5 us -> 0.8 us
  Pallas kernels: 0 us -> 22.5 us
  loops' own time: 8.35 us -> 0 us
    dot_general x48 -> x0, matrix products: 137 us -> none  [the longest x12 52.5 us: tile_grads(): jnp.einsum('gij,igd->jd', dscore, query_head, preferred_element_type=jnp....]
    ppermute x11 -> x0, starting transfers between devices: 98.1 us -> none  [partner_2(): return lax.ppermute(block, axis, route)]
    all_gather x1 -> x0, blocking collectives: 84.7 us -> none  [sent_together(): lax.all_gather(both, axis, axis=dim, tiled=True)]
    all_to_all x4 -> x2, starting transfers between devices: 96.2 us -> 12.7 us  [the longest x1 8.67 us: per_device(): lax.all_to_all(spread, 'seq', 0, 0, tiled=True).reshape(trunk, 2 * width)]
    sub x12 -> x0, matrix products: 28.1 us -> none  [tile_grads(): exponent = jnp.where(allowed[None], jnp.exp(scores - row_peak), 0.0)]
    pallas_call x0 -> x2, Pallas kernels: none -> 22.5 us  [the longest x1 14.3 us: per_device(): pl.pallas_call(lambda *refs: score_kernel(*refs, tiles=tiles), in_specs=[...]
    dynamic_slice x17 -> x0, local copies, waits for them, and re-layouts: 12.8 us -> none  [the longest x11 6.47 us: per_device(): own_sums, tile_outputs = lax.scan(one_slot, initial_sums, slot_entries)]
    dynamic_update_slice x8 -> x0, local copies, waits for them, and re-layouts: 11 us -> none  [per_device(): own_sums, tile_outputs = lax.scan(one_slot, initial_sums, slot_entries)]
  transfers between devices with their start and end apart: 15 -> 2, of which waited for: 3 -> 2; matrix products, arithmetic and copies ran while one was open for 44% -> 5% of each run, Pallas kernels for 0% -> 16%
where the time goes in v1:
time: 53 us; the launch traced here: 52.5 us
  Pallas kernels  22.5 us (42%)
  starting transfers between devices  12.7 us (24%)
  waiting for transfers between devices  10.9 us (21%)
  local copies, waits for them, and re-layouts  4.96 us (9%)
  other arithmetic  0.8 us (2%)
  between operations  0.67 us (1%)
    pallas_call x1, Pallas kernels, per_device(): pl.pallas_call(lambda *refs: score_kernel(*refs, tiles=tiles), in_specs=[...  14.3 us
    all_to_all x1, waiting for transfers between devices, per_device(): lax.all_to_all(spread, 'seq', 0, 0, tiled=True).reshape(trunk, 2 * width)  8.82 us
    all_to_all x1, starting transfers between devices, per_device(): lax.all_to_all(spread, 'seq', 0, 0, tiled=True).reshape(trunk, 2 * width)  8.67 us
    pallas_call x1, Pallas kernels, per_device(): pl.pallas_call(lambda *refs: grad_kernel(*refs, tiles=tiles), in_specs=[h...  8.14 us
    all_to_all x1, starting transfers between devices, per_device(): shares = lax.all_to_all(sums, 'seq', 0, 0, tiled=True)  4.06 us
    unnamed x4, local copies, waits for them, and re-layouts  3.49 us
    all_to_all x1, waiting for transfers between devices, per_device(): shares = lax.all_to_all(sums, 'seq', 0, 0, tiled=True)  2.03 us
  transfers between devices with their start and end apart: 2, of which 2 were waited for; matrix products, arithmetic and copies ran while one was open for 5% of the time, Pallas kernels for 16%

profile of v1, /device:TPU:64, one launch (start us, length us, event | category | flops | bytes accessed | tf_op | source)
XLA Modules:
  0.0 52.5 jit_solution(17156571847372037898)
XLA Ops:
  0.6 0.7 %pad_maximum_fusion = bf16[8,1024]{1,0:T(8,128)(2,1)S(1)} fusion(bf16[8,512]{1,0:T(8,128)(2,1)} %bitcast.18, bf16[8,512]{1,0:T(8,128)(2,1)} %bitcast.19), kind=kLoop, calls=%fused_computation.1 | loop fusion | flops 32768 | bytes 32768 | tf_op jit(solution)/shard_map/concatenate | solution.py:302
  1.3 0.9 %broadcast_in_dim.15 = bf16[32,8,1024]{2,1,0:T(8,128)(2,1)} broadcast(bf16[8,1024]{1,0:T(8,128)(2,1)S(1)} %pad_maximum_fusion), dimensions={1,2} | broadcast | bytes 540672 | tf_op jit(solution)/shard_map/broadcast_in_dim | solution.py:303
  2.2 8.7 %all-to-all-start = ((bf16[32,8,1024]{2,1,0:T(8,128)(2,1)}), bf16[32,8,1024]{2,1,0:T(8,128)(2,1)S(1)}, u32[]{:S(2)}, u32[]{:S(2)}) async-start(bf16[32,8,1024]{2,1,0:T(8,128)(2,1)} %broadcast_in_dim.15), calls=%async_computation | async-start | bytes 1048576 | tf_op jit(solution)/shard_map/all_to_all | solution.py:304
  10.9 1.4 %copy.13.refs_1_ = s32[8,4]{1,0:T(8,128)} copy(s32[8,4]{0,1:T(4,128)} %param.14) | data formatting | bytes 256 | tf_op args[6]
  12.2 1.3 %copy.14.refs_2_ = s32[8,4]{1,0:T(8,128)} copy(s32[8,4]{0,1:T(4,128)} %param.15) | data formatting | bytes 256 | tf_op args[7]
  13.6 8.8 %all-to-all-done = bf16[32,8,1024]{2,1,0:T(8,128)(2,1)S(1)} async-done(((bf16[32,8,1024]{2,1,0:T(8,128)(2,1)}), bf16[32,8,1024]{2,1,0:T(8,128)(2,1)S(1)}, u32[]{:S(2)}, u32[]{:S(2)}) %all-to-all-start) | async-done | bytes 524320 | tf_op jit(solution)/shard_map/all_to_all | solution.py:304
  22.4 0.0 copy-start
  22.4 0.8 %copy-done = bf16[32,8,1024]{2,1,0:T(8,128)(2,1)} copy-done((bf16[32,8,1024]{2,1,0:T(8,128)(2,1)}, bf16[32,8,1024]{2,1,0:T(8,128)(2,1)S(1)}, u32[]{:S(2)}) %copy-start) | copy-done | bytes 524312
  23.2 14.3 %scores.1 = (bf16[32,2,8,512]{3,2,1,0:T(8,128)(2,1)}, bf16[4,4,320,512]{3,2,1,0:T(8,128)(2,1)}, bf16[4,4,64,512]{3,2,1,0:T(8,128)(2,1)}, bf16[256,1024]{1,0:T(8,128)(2,1)}) custom-call(s32[1]{0:T(128)} %bitcast.2.refs_0_, s32[8,4]{1,0:T(8,128)} %copy.13.refs_1_, s32[8,4]{1,0:T(8,128)} %copy.14.refs_2_, bf16[256,4096]{1,0:T(8,128)(2,1)} %bitcast.11, ...), custom_call_target="tpu_custom_call" | custom-call | flops 2684354560 | bytes 12582912 | tf_op jit(solution)/shard_map/scores/pallas_call | solution.py:313
  37.5 4.1 %all-to-all-start.1 = ((bf16[32,2,8,512]{3,2,1,0:T(8,128)(2,1)}), bf16[32,2,8,512]{3,2,1,0:T(8,128)(2,1)S(1)}, u32[]{:S(2)}, u32[]{:S(2)}) async-start(bf16[32,2,8,512]{3,2,1,0:T(8,128)(2,1)} %get-tuple-element.18), calls=%async_computation.1 | async-start | bytes 1048576 | tf_op jit(solution)/shard_map/all_to_all | solution.py:341
  41.6 8.1 %grads.1 = (f32[256,4096]{1,0:T(8,128)}, f32[256,512]{1,0:T(8,128)}, f32[256,512]{1,0:T(8,128)}) custom-call(bf16[256,4096]{1,0:T(8,128)(2,1)} %bitcast.12, bf16[256,4096]{1,0:T(8,128)(2,1)} %bitcast.14, bf16[256,1024]{1,0:T(8,128)(2,1)} %get-tuple-element.12.refs_2_, bf16[256,512]{1,0:T(8,128)(2,1)} %bitcast.17, ...), custom_call_target="tpu_custom_call" | custom-call | flops 1342177280 | bytes 16777216 | tf_op jit(solution)/shard_map/grads/pallas_call | solution.py:343
  49.8 2.0 %all-to-all-done.1 = bf16[32,2,8,512]{3,2,1,0:T(8,128)(2,1)S(1)} async-done(((bf16[32,2,8,512]{3,2,1,0:T(8,128)(2,1)}), bf16[32,2,8,512]{3,2,1,0:T(8,128)(2,1)S(1)}, u32[]{:S(2)}, u32[]{:S(2)}) %all-to-all-start.1) | async-done | bytes 524320 | tf_op jit(solution)/shard_map/all_to_all | solution.py:341
  51.8 0.1 convert_reduce_fusion
  51.9 0.6 %fusion = (f32[1,8,512]{2,1,0:T(8,128)}, f32[1,8,512]{2,1,0:T(8,128)}) fusion(f32[2,8,512]{2,1,0:T(8,128)S(1)} %convert_reduce_fusion), kind=kLoop, calls=%fused_computation.2 | loop fusion | bytes 65536 | tf_op jit(solution)/shard_map/slice | solution.py:370
Async XLA Ops:
  2.2 20.2 %all-to-all-start = ((bf16[32,8,1024]{2,1,0:T(8,128)(2,1)}), bf16[32,8,1024]{2,1,0:T(8,128)(2,1)S(1)}, u32[]{:S(2)}, u32[]{:S(2)}) async-start(bf16[32,8,1024]{2,1,0:T(8,128)(2,1)} %broadcast_in_dim.15), calls=%async_computation | async-start | bytes 1048576 | tf_op jit(solution)/shard_map/all_to_all | solution.py:304
  22.4 0.8 %copy-start = (bf16[32,8,1024]{2,1,0:T(8,128)(2,1)}, bf16[32,8,1024]{2,1,0:T(8,128)(2,1)S(1)}, u32[]{:S(2)}) copy-start(bf16[32,8,1024]{2,1,0:T(8,128)(2,1)S(1)} %all-to-all-done) | copy-start | bytes 1572868
  37.5 14.3 %all-to-all-start.1 = ((bf16[32,2,8,512]{3,2,1,0:T(8,128)(2,1)}), bf16[32,2,8,512]{3,2,1,0:T(8,128)(2,1)S(1)}, u32[]{:S(2)}, u32[]{:S(2)}) async-start(bf16[32,2,8,512]{3,2,1,0:T(8,128)(2,1)} %get-tuple-element.18), calls=%async_computation.1 | async-start | bytes 1048576 | tf_op jit(solution)/shard_map/all_to_all | solution.py:341

commit v2 on v1

v2 whole, which is shorter than its diff:
```python
import math

import jax
import jax.numpy as jnp
from jax import lax
from jax.experimental import pallas as pl
from jax.experimental.pallas import tpu as pltpu
from jax.sharding import PartitionSpec as P

HEAD_SIZE = 128
MASKED = -1e30
CHUNK = 256


def dot_nt(a, b):
    return lax.dot_general(a, b, (((1,), (1,)), ((), ())), preferred_element_type=jnp.float32)


def dot_tn(a, b):
    return lax.dot_general(a, b, (((0,), (0,)), ((), ())), preferred_element_type=jnp.float32)


def dot_nn(a, b):
    return lax.dot_general(a, b, (((1,), (0,)), ((), ())), preferred_element_type=jnp.float32)


def lanes(start):
    if isinstance(start, int):
        return slice(start, start + HEAD_SIZE)
    return pl.ds(pl.multiple_of(start, HEAD_SIZE), HEAD_SIZE)


def iota(shape, dim):
    return lax.broadcasted_iota(jnp.int32, shape, dim)


def stacked(ref, h, tile, first, count):
    return jnp.concatenate(
        [ref[h, tile, lanes((first + j) * HEAD_SIZE)] for j in range(count)], axis=0
    )


def head_fetches(h, q_hbm, do_hbm, q, do, sems):
    width = q.shape[2]
    span = pl.ds(pl.multiple_of(h * width, width), width)
    return [
        pltpu.make_async_copy(q_hbm.at[:, span], q.at[h], sems.at[0, h]),
        pltpu.make_async_copy(do_hbm.at[:, span], do.at[h], sems.at[1, h]),
    ]


def mask_of_queries(rows):
    shape = (CHUNK, HEAD_SIZE)
    column, row = iota(shape, 1), jnp.bitwise_and(iota(shape, 0), rows - 1)
    return jnp.where(
        column < rows,
        jnp.where(column > row, MASKED, 0.0),
        jnp.where(column == rows, 1.0, 0.0),
    ).astype(jnp.bfloat16)


def local_kernel(
    q_hbm,
    do_hbm,
    kb_hbm,
    vb_hbm,
    e_hbm,
    g_hbm,
    stats_hbm,
    q,
    do,
    kb,
    vb,
    e_buf,
    g_buf,
    stats,
    query_mask,
    sems_in,
    sems_out,
    *,
    tiles,
):
    rows = q_hbm.shape[0] // tiles
    heads = q.shape[0]
    per_chunk = CHUNK // rows
    halves = q.shape[2] // (per_chunk * HEAD_SIZE)
    to_exp2 = math.log2(math.e) / math.sqrt(HEAD_SIZE)
    branch_fetches = [
        pltpu.make_async_copy(kb_hbm, kb, sems_in.at[0, heads]),
        pltpu.make_async_copy(vb_hbm, vb, sems_in.at[1, heads]),
    ]
    for copy in branch_fetches:
        copy.start()
    for h in range(heads):
        for copy in head_fetches(h, q_hbm, do_hbm, q, do, sems_in):
            copy.start()
    query_mask[...] = mask_of_queries(rows)
    shape = (rows, HEAD_SIZE)
    one_hot = jnp.where(iota(shape, 0) == iota(shape, 1), 1.0, 0.0).astype(jnp.bfloat16)
    for copy in branch_fetches:
        copy.wait()

    def stores(h):
        used = slice(0, stats.shape[2])
        return [
            pltpu.make_async_copy(e_buf.at[:, h], e_hbm.at[:, h], sems_out.at[0, h]),
            pltpu.make_async_copy(g_buf.at[:, h], g_hbm.at[:, h], sems_out.at[1, h]),
            pltpu.make_async_copy(stats.at[:, h], stats_hbm.at[:, h, used], sems_out.at[2, h]),
        ]

    def head_step(h, carry):
        for copy in head_fetches(h, q_hbm, do_hbm, q, do, sems_in):
            copy.wait()
        span = lanes(h * HEAD_SIZE)
        for t in range(tiles):
            tile = slice(t * rows, (t + 1) * rows)
            for half in range(halves):
                queries = stacked(q, h, tile, half * per_chunk, per_chunk)
                grads = stacked(do, h, tile, half * per_chunk, per_chunk)
                score = dot_nt(
                    jnp.concatenate([kb[tile, span], one_hot], axis=1),
                    jnp.concatenate([queries, query_mask[...]], axis=1),
                )
                grad = dot_nt(vb[tile, span], grads)
                peak = jnp.max(score, axis=0, keepdims=True)
                e = jnp.exp2((score - peak) * to_exp2)
                part = slice(half * CHUNK, (half + 1) * CHUNK)
                e_buf[t, h, :, part] = e.astype(jnp.bfloat16)
                g_buf[t, h, :, part] = grad.astype(jnp.bfloat16)
                stats[t, h, 0:1, part] = peak
                stats[t, h, 1:2, part] = jnp.sum(e, axis=0, keepdims=True)
                stats[t, h, 2:3, part] = jnp.sum(e * grad, axis=0, keepdims=True)
                stats[t, h, 3:, part] = jnp.zeros((stats.shape[2] - 3, CHUNK), jnp.float32)
        for copy in stores(h):
            copy.start()
        return carry

    lax.fori_loop(0, heads, head_step, 0)
    for h in range(heads):
        for copy in stores(h):
            copy.wait()


def score_kernel(
    leaf,
    lengths,
    parents,
    q_hbm,
    do_hbm,
    kv,
    stats_hbm,
    sums_hbm,
    ds_hbm,
    rows_hbm,
    q,
    do,
    stats,
    sums,
    ds_buf,
    row_buf,
    low_buf,
    key_mask,
    query_mask,
    sems_in,
    sems_out,
    *,
    tiles,
):
    rows = q_hbm.shape[0] // tiles
    trunk = kv.shape[0]
    width = kv.shape[1] // 2
    heads = width // HEAD_SIZE
    group_width = q_hbm.shape[1] // heads
    per_chunk = CHUNK // rows
    halves = group_width // (per_chunk * HEAD_SIZE)
    scale = 1.0 / math.sqrt(HEAD_SIZE)
    to_exp2 = scale * math.log2(math.e)
    tree = leaf[0]

    def fetches(h):
        return head_fetches(h, q_hbm, do_hbm, q, do, sems_in)

    def tile_stores(h, t):
        return [
            pltpu.make_async_copy(ds_buf.at[t, h], ds_hbm.at[t * heads + h], sems_out.at[0, h, t]),
            pltpu.make_async_copy(
                row_buf.at[t, h],
                rows_hbm.at[t, h, 0 : row_buf.shape[2]],
                sems_out.at[1, h, t],
            ),
        ]

    def sum_store(h):
        span = lanes(h * HEAD_SIZE)
        return pltpu.make_async_copy(
            sums.at[h], sums_hbm.at[:, :, :, span], sems_out.at[2, h, 0]
        )

    kv_stores = [
        pltpu.make_async_copy(
            kv.at[:, i * width : (i + 1) * width],
            ds_hbm.at[tiles * heads + i],
            sems_out.at[2, i, 1],
        )
        for i in range(2)
    ]
    stats_fetch = pltpu.make_async_copy(
        stats_hbm.at[:, :, 0 : stats.shape[2]], stats, sems_in.at[0, heads]
    )
    for copy in fetches(0):
        copy.start()
    stats_fetch.start()
    for copy in kv_stores:
        copy.start()

    query_mask[...] = mask_of_queries(rows)
    shape = (trunk, HEAD_SIZE)
    column, row = iota(shape, 1), iota(shape, 0)
    for t in range(tiles):
        key_mask[t] = jnp.where(
            (column == rows) & (row > parents[tree, t]), MASKED, 0.0
        ).astype(jnp.bfloat16)
    lane_row = jnp.bitwise_and(iota((1, CHUNK), 1), rows - 1)
    live = [jnp.where(lane_row < lengths[tree, t], 1.0, 0.0) for t in range(tiles)]

    stats_fetch.wait()

    def matmuls(h, t, half):
        tile = slice(t * rows, (t + 1) * rows)
        queries = stacked(q, h, tile, half * per_chunk, per_chunk)
        grads = stacked(do, h, tile, half * per_chunk, per_chunk)
        scores = dot_nt(
            jnp.concatenate([kv[:, lanes(h * HEAD_SIZE)], key_mask[t]], axis=1),
            jnp.concatenate([queries, query_mask[...]], axis=1),
        )
        return scores, dot_nt(kv[:, lanes(width + h * HEAD_SIZE)], grads)

    def softmax(h, t, half, score, grad):
        part = slice(half * CHUNK, (half + 1) * CHUNK)
        branch_peak = stats[t, h, 0:1, part]
        peak = jnp.maximum(jnp.max(score, axis=0, keepdims=True), branch_peak)
        e = jnp.exp2((score - peak) * to_exp2)
        shrink = jnp.exp2((branch_peak - peak) * to_exp2)
        inv = live[t] / (jnp.sum(e, axis=0, keepdims=True) + shrink * stats[t, h, 1:2, part])
        delta = inv * (
            jnp.sum(e * grad, axis=0, keepdims=True) + shrink * stats[t, h, 2:3, part]
        )
        weights = e * inv
        ds_buf[t, h, :, part] = (weights * (grad - delta)).astype(jnp.bfloat16)
        low_buf[t, :, part] = weights.astype(jnp.bfloat16)
        row_buf[t, h, 0:1, part] = shrink * inv
        row_buf[t, h, 1:2, part] = delta
        row_buf[t, h, 2:, part] = jnp.zeros((row_buf.shape[2] - 2, CHUNK), jnp.float32)

    def trunk_parts(h, t):
        count = per_chunk * halves
        tile = slice(t * rows, (t + 1) * rows)
        left = jnp.concatenate([ds_buf[t, h], low_buf[t]], axis=0)
        right = jnp.concatenate(
            [stacked(q, h, tile, 0, count), stacked(do, h, tile, 0, count)], axis=1
        )
        both = dot_nn(left, right)
        return both[:trunk, :HEAD_SIZE], both[trunk:, HEAD_SIZE:]

    order = [(t, half) for t in range(tiles) for half in range(halves)]

    def head_step(h, carry):
        totals = None
        for copy in fetches(h):
            copy.wait()

        @pl.when(h + 1 < heads)
        def _():
            for copy in fetches(h + 1):
                copy.start()

        ahead = matmuls(h, *order[0])
        for c, (t, half) in enumerate(order):
            now = ahead
            if c + 1 < len(order):
                ahead = matmuls(h, *order[c + 1])
            softmax(h, t, half, *now)
            if half == halves - 1:
                parts = trunk_parts(h, t)
                totals = parts if t == 0 else tuple(a + b for a, b in zip(totals, parts))
                for copy in tile_stores(h, t):
                    copy.start()
        shape = (sums.shape[1], sums.shape[3], HEAD_SIZE)
        sums[h, :, 0] = (totals[0] * scale).reshape(shape).astype(jnp.bfloat16)
        sums[h, :, 1] = totals[1].reshape(shape).astype(jnp.bfloat16)
        sum_store(h).start()
        return carry

    lax.fori_loop(0, heads, head_step, 0)
    for copy in kv_stores:
        copy.wait()
    for h in range(heads):
        sum_store(h).wait()
        for t in range(tiles):
            for copy in tile_stores(h, t):
                copy.wait()


def grad_kernel(
    q_hbm,
    do_hbm,
    kb_hbm,
    ds_hbm,
    e_hbm,
    g_hbm,
    rows_hbm,
    dq,
    dkb,
    dvb,
    q,
    do,
    kv,
    kb,
    ds,
    e,
    g,
    row_values,
    dq_buf,
    dkb_buf,
    dvb_buf,
    sems_in,
    sems,
    *,
    tiles,
):
    rows = q_hbm.shape[0] // tiles
    width = kb_hbm.shape[1]
    heads = width // HEAD_SIZE
    group_width = q_hbm.shape[1] // heads
    groups = group_width // HEAD_SIZE
    scale = 1.0 / math.sqrt(HEAD_SIZE)

    def fetches(t):
        tile = pl.ds(pl.multiple_of(t * rows, rows), rows)
        return [
            pltpu.make_async_copy(source.at[part], buf.at[part], sems_in.at[i, t])
            for i, (source, buf, part) in enumerate(
                (
                    (q_hbm, q, tile),
                    (do_hbm, do, tile),
                    (e_hbm, e, t),
                    (g_hbm, g, t),
                    (kb_hbm, kb, tile),
                )
            )
        ]

    kv_fetches = [
        pltpu.make_async_copy(
            ds_hbm.at[tiles * heads + i],
            kv.at[:, i * width : (i + 1) * width],
            sems_in.at[7, i],
        )
        for i in range(2)
    ]
    for copy in kv_fetches:
        copy.start()
    def computed_fetches(t):
        return [
            pltpu.make_async_copy(
                ds_hbm.at[pl.ds(pl.multiple_of(t * heads, heads), heads)],
                ds.at[t],
                sems_in.at[5, t],
            ),
            pltpu.make_async_copy(
                rows_hbm.at[t, :, 0 : row_values.shape[2]], row_values.at[t], sems_in.at[6, t]
            ),
        ]

    for t in range(tiles):
        for copy in fetches(t) + computed_fetches(t):
            copy.start()
    for copy in kv_fetches:
        copy.wait()

    def copies(t):
        tile = pl.ds(pl.multiple_of(t * rows, rows), rows)
        return [
            pltpu.make_async_copy(buf.at[tile], out.at[tile], sems.at[i, t])
            for i, (buf, out) in enumerate(((dq_buf, dq), (dkb_buf, dkb), (dvb_buf, dvb)))
        ]

    def tile_step(t, carry):
        for copy in fetches(t) + computed_fetches(t):
            copy.wait()
        tile = pl.ds(pl.multiple_of(t * rows, rows), rows)

        def all_heads(ref, h):
            return jnp.concatenate(
                [ref[tile, lanes(h * group_width + j * HEAD_SIZE)] for j in range(groups)], axis=0
            )

        for h in range(heads):
            span = lanes(h * HEAD_SIZE)
            keys = jnp.concatenate([kv[:, span], kb[tile, span]], axis=0)
            weights = e[t, h].astype(jnp.float32) * row_values[t, h, 0:1, :]
            branch_ds = weights * (g[t, h].astype(jnp.float32) - row_values[t, h, 1:2, :])
            branch_ds = branch_ds.astype(jnp.bfloat16)
            dkb_buf[tile, span] = dot_nn(branch_ds, all_heads(q, h)) * scale
            dvb_buf[tile, span] = dot_nn(weights.astype(jnp.bfloat16), all_heads(do, h))
            got = (dot_tn(keys, jnp.concatenate([ds[t, h], branch_ds], axis=0)) * scale).T
            for j in range(groups):
                dq_buf[tile, lanes(h * group_width + j * HEAD_SIZE)] = got[
                    j * rows : (j + 1) * rows
                ]
        for copy in copies(t):
            copy.start()
        return carry

    lax.fori_loop(0, tiles, tile_step, 0)
    for t in range(tiles):
        for copy in copies(t):
            copy.wait()


def per_device(
    queries,
    branch_key_rows,
    branch_value_rows,
    grad_output,
    trunk_keys,
    trunk_token_values,
    lengths,
    parents,
):
    q = queries[0]
    do = grad_output[0]
    kb = branch_key_rows[0]
    vb = branch_value_rows[0]
    seq = lax.axis_size("seq")
    leaf = lax.axis_index("leaf").astype(jnp.int32).reshape(1)
    tiles = lengths.shape[1]
    rows = q.shape[0] // tiles
    width = kb.shape[1]
    heads = width // HEAD_SIZE
    wide = q.shape[1] // width * rows
    own = trunk_keys.shape[1]
    trunk = own * seq
    work = heads * tiles * wide * (trunk + rows) * HEAD_SIZE * 2

    both = jnp.concatenate([trunk_keys[0], trunk_token_values[0]], axis=1)
    spread = jnp.broadcast_to(both[None], (seq,) + both.shape)
    gathered = lax.all_to_all(spread, "seq", 0, 0, tiled=True).reshape(trunk, 2 * width)

    vmem = pl.BlockSpec(memory_space=pltpu.VMEM)
    smem = pl.BlockSpec(memory_space=pltpu.SMEM)
    hbm = pl.BlockSpec(memory_space=pltpu.HBM)
    ds_shape = (tiles, heads, trunk, wide)
    branch_shape = (tiles, heads, rows, wide)
    stats_shape = (tiles, heads, 8, wide)
    kept_shape = (tiles, heads, rows + 16, wide)
    head_shape = (heads, tiles * rows, q.shape[1] // heads)

    e, g, stats = pl.pallas_call(
        lambda *refs: local_kernel(*refs, tiles=tiles),
        in_specs=[hbm] * 4,
        out_specs=[hbm] * 3,
        out_shape=[
            jax.ShapeDtypeStruct(branch_shape, jnp.bfloat16),
            jax.ShapeDtypeStruct(branch_shape, jnp.bfloat16),
            jax.ShapeDtypeStruct(kept_shape, jnp.float32),
        ],
        scratch_shapes=[
            pltpu.VMEM(head_shape, jnp.bfloat16),
            pltpu.VMEM(head_shape, jnp.bfloat16),
            pltpu.VMEM(kb.shape, jnp.bfloat16),
            pltpu.VMEM(vb.shape, jnp.bfloat16),
            pltpu.VMEM(branch_shape, jnp.bfloat16),
            pltpu.VMEM(branch_shape, jnp.bfloat16),
            pltpu.VMEM(stats_shape, jnp.float32),
            pltpu.VMEM((CHUNK, HEAD_SIZE), jnp.bfloat16),
            pltpu.SemaphoreType.DMA((2, heads + 1)),
            pltpu.SemaphoreType.DMA((3, heads)),
        ],
        compiler_params=pltpu.CompilerParams(vmem_limit_bytes=65_900_000),
        cost_estimate=pl.CostEstimate(flops=2 * work, bytes_accessed=7 << 20, transcendentals=0),
        name="local",
    )(q, do, kb, vb)

    sums, ds, row_values = pl.pallas_call(
        lambda *refs: score_kernel(*refs, tiles=tiles),
        in_specs=[smem] * 3 + [hbm, hbm, vmem, hbm],
        out_specs=[hbm] * 3,
        out_shape=[
            jax.ShapeDtypeStruct((seq, 2, own, width), jnp.bfloat16),
            jax.ShapeDtypeStruct((tiles * heads + 2, trunk, wide), jnp.bfloat16),
            jax.ShapeDtypeStruct(kept_shape, jnp.float32),
        ],
        scratch_shapes=[
            pltpu.VMEM(head_shape, jnp.bfloat16),
            pltpu.VMEM(head_shape, jnp.bfloat16),
            pltpu.VMEM(stats_shape, jnp.float32),
            pltpu.VMEM((heads, seq, 2, own, HEAD_SIZE), jnp.bfloat16),
            pltpu.VMEM(ds_shape, jnp.bfloat16),
            pltpu.VMEM(stats_shape, jnp.float32),
            pltpu.VMEM((tiles, trunk, wide), jnp.bfloat16),
            pltpu.VMEM((tiles, trunk, HEAD_SIZE), jnp.bfloat16),
            pltpu.VMEM((CHUNK, HEAD_SIZE), jnp.bfloat16),
            pltpu.SemaphoreType.DMA((2, heads + 1)),
            pltpu.SemaphoreType.DMA((3, heads, tiles)),
        ],
        compiler_params=pltpu.CompilerParams(vmem_limit_bytes=53_500_000),
        cost_estimate=pl.CostEstimate(
            flops=4 * work, bytes_accessed=12 << 20, transcendentals=work // 256
        ),
        name="scores",
    )(leaf, lengths, parents, q, do, gathered, stats)

    shares = lax.all_to_all(sums, "seq", 0, 0, tiled=True)

    dq, dkb, dvb = pl.pallas_call(
        lambda *refs: grad_kernel(*refs, tiles=tiles),
        in_specs=[hbm] * 7,
        out_specs=[hbm] * 3,
        out_shape=[
            jax.ShapeDtypeStruct(q.shape, jnp.float32),
            jax.ShapeDtypeStruct(kb.shape, jnp.float32),
            jax.ShapeDtypeStruct(vb.shape, jnp.float32),
        ],
        scratch_shapes=[
            pltpu.VMEM(q.shape, jnp.bfloat16),
            pltpu.VMEM(q.shape, jnp.bfloat16),
            pltpu.VMEM(gathered.shape, jnp.bfloat16),
            pltpu.VMEM(kb.shape, jnp.bfloat16),
            pltpu.VMEM(ds_shape, jnp.bfloat16),
            pltpu.VMEM(branch_shape, jnp.bfloat16),
            pltpu.VMEM(branch_shape, jnp.bfloat16),
            pltpu.VMEM(stats_shape, jnp.float32),
            pltpu.VMEM(q.shape, jnp.float32),
            pltpu.VMEM(kb.shape, jnp.float32),
            pltpu.VMEM(vb.shape, jnp.float32),
            pltpu.SemaphoreType.DMA((8, tiles)),
            pltpu.SemaphoreType.DMA((3, tiles)),
        ],
        compiler_params=pltpu.CompilerParams(vmem_limit_bytes=65_900_000),
        cost_estimate=pl.CostEstimate(flops=2 * work, bytes_accessed=16 << 20, transcendentals=0),
        name="grads",
    )(q, do, kb, ds, e, g, row_values)

    trunk_grads = jnp.sum(shares.astype(jnp.float32), axis=0)
    return dq[None], dkb[None], dvb[None], trunk_grads[0][None], trunk_grads[1][None]


def solution(mesh):
    split = P("leaf", "seq", None)
    return jax.shard_map(
        per_device,
        mesh=mesh,
        in_specs=(split,) * 6 + (P(None, "seq"),) * 2,
        out_specs=(split,) * 5,
        check_vma=False,
    )
```

time: 53 us -> 49.6 us (0.936)
  waiting for transfers between devices: 10.9 us -> 7.76 us
  local copies, waits for them, and re-layouts: 4.96 us -> 2.98 us
  Pallas kernels: 22.5 us -> 24.1 us
    pallas_call x0 -> x1, Pallas kernels: none -> 4.92 us  [per_device(): pl.pallas_call(lambda *refs: local_kernel(*refs, tiles=tiles), in_specs=[...]
    all_to_all x1, waiting for transfers between devices: 8.82 us -> 5.08 us  [per_device(): lax.all_to_all(spread, 'seq', 0, 0, tiled=True).reshape(trunk, 2 * width)]
    pallas_call x1, Pallas kernels: 14.3 us -> 11.6 us  [per_device(): pl.pallas_call(lambda *refs: score_kernel(*refs, tiles=tiles), in_specs=[...]
    unnamed x4 -> x2, local copies, waits for them, and re-layouts: 3.49 us -> 1.51 us
    all_to_all x1, waiting for transfers between devices: 2.03 us -> 2.68 us  [per_device(): shares = lax.all_to_all(sums, 'seq', 0, 0, tiled=True)]
    pallas_call x1, Pallas kernels: 8.14 us -> 7.51 us  [per_device(): pl.pallas_call(lambda *refs: grad_kernel(*refs, tiles=tiles), in_specs=[h...]
  transfers between devices with their start and end apart: 2 -> 2, of which waited for: 2 -> 2; matrix products, arithmetic and copies ran while one was open for 5% -> 3% of each run, Pallas kernels for 16% -> 25%
where the time goes in v2:
time: 49.6 us; the launch traced here: 49 us
  Pallas kernels  24.1 us (49%)
  starting transfers between devices  12.7 us (26%)
  waiting for transfers between devices  7.76 us (16%)
  local copies, waits for them, and re-layouts  2.98 us (6%)
  other arithmetic  0.8 us (2%)
  between operations  0.68 us (1%)
    pallas_call x1, Pallas kernels, per_device(): pl.pallas_call(lambda *refs: score_kernel(*refs, tiles=tiles), in_specs=[...  11.6 us
    all_to_all x1, starting transfers between devices, per_device(): lax.all_to_all(spread, 'seq', 0, 0, tiled=True).reshape(trunk, 2 * width)  8.67 us
    pallas_call x1, Pallas kernels, per_device(): pl.pallas_call(lambda *refs: grad_kernel(*refs, tiles=tiles), in_specs=[h...  7.51 us
    all_to_all x1, waiting for transfers between devices, per_device(): lax.all_to_all(spread, 'seq', 0, 0, tiled=True).reshape(trunk, 2 * width)  5.08 us
    pallas_call x1, Pallas kernels, per_device(): pl.pallas_call(lambda *refs: local_kernel(*refs, tiles=tiles), in_specs=[...  4.92 us
    all_to_all x1, starting transfers between devices, per_device(): shares = lax.all_to_all(sums, 'seq', 0, 0, tiled=True)  4.06 us
    all_to_all x1, waiting for transfers between devices, per_device(): shares = lax.all_to_all(sums, 'seq', 0, 0, tiled=True)  2.68 us
    unnamed x2, local copies, waits for them, and re-layouts  1.51 us
  transfers between devices with their start and end apart: 2, of which 2 were waited for; matrix products, arithmetic and copies ran while one was open for 3% of the time, Pallas kernels for 25%

profile of v2, /device:TPU:64, one launch (start us, length us, event | category | flops | bytes accessed | tf_op | source)
XLA Modules:
  0.0 49.0 jit_solution(14651993985925443534)
XLA Ops:
  0.6 0.7 %pad_maximum_fusion = bf16[8,1024]{1,0:T(8,128)(2,1)S(1)} fusion(bf16[8,512]{1,0:T(8,128)(2,1)} %bitcast.20, bf16[8,512]{1,0:T(8,128)(2,1)} %bitcast.21), kind=kLoop, calls=%fused_computation.1 | loop fusion | flops 32768 | bytes 32768 | tf_op jit(solution)/shard_map/concatenate | solution.py:446
  1.3 0.9 %broadcast_in_dim.15 = bf16[32,8,1024]{2,1,0:T(8,128)(2,1)} broadcast(bf16[8,1024]{1,0:T(8,128)(2,1)S(1)} %pad_maximum_fusion), dimensions={1,2} | broadcast | bytes 540672 | tf_op jit(solution)/shard_map/broadcast_in_dim | solution.py:447
  2.2 8.7 %all-to-all-start = ((bf16[32,8,1024]{2,1,0:T(8,128)(2,1)}), bf16[32,8,1024]{2,1,0:T(8,128)(2,1)S(1)}, u32[]{:S(2)}, u32[]{:S(2)}) async-start(bf16[32,8,1024]{2,1,0:T(8,128)(2,1)} %broadcast_in_dim.15), calls=%async_computation | async-start | bytes 1048576 | tf_op jit(solution)/shard_map/all_to_all | solution.py:448
  10.9 0.8 %copy.13.refs_1_ = s32[8,4]{1,0:T(8,128)S(1)} copy(s32[8,4]{0,1:T(4,128)} %param.14) | data formatting | bytes 256 | tf_op args[6]
  11.6 0.8 %copy.14.refs_2_ = s32[8,4]{1,0:T(8,128)S(1)} copy(s32[8,4]{0,1:T(4,128)} %param.15) | data formatting | bytes 256 | tf_op args[7]
  12.4 4.9 %local.1 = (bf16[4,4,64,512]{3,2,1,0:T(8,128)(2,1)}, bf16[4,4,64,512]{3,2,1,0:T(8,128)(2,1)}, f32[4,4,80,512]{3,2,1,0:T(8,128)}) custom-call(bf16[256,4096]{1,0:T(8,128)(2,1)} %bitcast.12, bf16[256,4096]{1,0:T(8,128)(2,1)} %bitcast.15, bf16[256,512]{1,0:T(8,128)(2,1)} %bitcast.18, bf16[256,512]{1,0:T(8,128)(2,1)} %bitcast.25), custom_call_target="tpu_custom_call" | custom-call | flops 1342177280 | bytes 7340032 | tf_op jit(solution)/shard_map/local/pallas_call | solution.py:459
  17.3 5.1 %all-to-all-done = bf16[32,8,1024]{2,1,0:T(8,128)(2,1)S(1)} async-done(((bf16[32,8,1024]{2,1,0:T(8,128)(2,1)}), bf16[32,8,1024]{2,1,0:T(8,128)(2,1)S(1)}, u32[]{:S(2)}, u32[]{:S(2)}) %all-to-all-start) | async-done | bytes 524320 | tf_op jit(solution)/shard_map/all_to_all | solution.py:448
  22.4 11.6 %scores.1 = (bf16[32,2,8,512]{3,2,1,0:T(8,128)(2,1)}, bf16[18,256,512]{2,1,0:T(8,128)(2,1)}, f32[4,4,80,512]{3,2,1,0:T(8,128)}) custom-call(s32[1]{0:T(128)} %bitcast.3.refs_0_, s32[8,4]{1,0:T(8,128)S(1)} %copy.13.refs_1_, s32[8,4]{1,0:T(8,128)S(1)} %copy.14.refs_2_, bf16[256,4096]{1,0:T(8,128)(2,1)} %bitcast.13, bf16[256,4096]{1,0:T(8,128)(2,1)} %bitcast.16, ...), custom_call_target="tpu_custom_call" | custom-call | flops 2684354560 | bytes 12582912 | tf_op jit(solution)/shard_map/scores/pallas_call | solution.py:485
  34.1 4.1 %all-to-all-start.1 = ((bf16[32,2,8,512]{3,2,1,0:T(8,128)(2,1)}), bf16[32,2,8,512]{3,2,1,0:T(8,128)(2,1)S(1)}, u32[]{:S(2)}, u32[]{:S(2)}) async-start(bf16[32,2,8,512]{3,2,1,0:T(8,128)(2,1)} %get-tuple-element.22), calls=%async_computation.1 | async-start | bytes 1048576 | tf_op jit(solution)/shard_map/all_to_all | solution.py:514
  38.1 7.5 %grads.1 = (f32[256,4096]{1,0:T(8,128)}, f32[256,512]{1,0:T(8,128)}, f32[256,512]{1,0:T(8,128)}) custom-call(bf16[256,4096]{1,0:T(8,128)(2,1)} %bitcast.14, bf16[256,4096]{1,0:T(8,128)(2,1)} %bitcast.17, bf16[256,512]{1,0:T(8,128)(2,1)} %bitcast.19, bf16[18,256,512]{2,1,0:T(8,128)(2,1)} %get-tuple-element.15.refs_3_, ...), custom_call_target="tpu_custom_call" | custom-call | flops 1342177280 | bytes 16777216 | tf_op jit(solution)/shard_map/grads/pallas_call | solution.py:516
  45.6 2.7 %all-to-all-done.1 = bf16[32,2,8,512]{3,2,1,0:T(8,128)(2,1)S(1)} async-done(((bf16[32,2,8,512]{3,2,1,0:T(8,128)(2,1)}), bf16[32,2,8,512]{3,2,1,0:T(8,128)(2,1)S(1)}, u32[]{:S(2)}, u32[]{:S(2)}) %all-to-all-start.1) | async-done | bytes 524320 | tf_op jit(solution)/shard_map/all_to_all | solution.py:514
  48.3 0.1 convert_reduce_fusion
  48.4 0.6 %fusion = (f32[1,8,512]{2,1,0:T(8,128)}, f32[1,8,512]{2,1,0:T(8,128)}) fusion(f32[2,8,512]{2,1,0:T(8,128)S(1)} %convert_reduce_fusion), kind=kLoop, calls=%fused_computation.2 | loop fusion | bytes 65536 | tf_op jit(solution)/shard_map/slice | solution.py:546
Async XLA Ops:
  2.2 20.2 %all-to-all-start = ((bf16[32,8,1024]{2,1,0:T(8,128)(2,1)}), bf16[32,8,1024]{2,1,0:T(8,128)(2,1)S(1)}, u32[]{:S(2)}, u32[]{:S(2)}) async-start(bf16[32,8,1024]{2,1,0:T(8,128)(2,1)} %broadcast_in_dim.15), calls=%async_computation | async-start | bytes 1048576 | tf_op jit(solution)/shard_map/all_to_all | solution.py:448
  34.1 14.3 %all-to-all-start.1 = ((bf16[32,2,8,512]{3,2,1,0:T(8,128)(2,1)}), bf16[32,2,8,512]{3,2,1,0:T(8,128)(2,1)S(1)}, u32[]{:S(2)}, u32[]{:S(2)}) async-start(bf16[32,2,8,512]{3,2,1,0:T(8,128)(2,1)} %get-tuple-element.22), calls=%async_computation.1 | async-start | bytes 1048576 | tf_op jit(solution)/shard_map/all_to_all | solution.py:514

commit v3 on v2

--- a/solution.py
+++ b/solution.py
@@ -281,10 +281,10 @@
                 ahead = matmuls(h, *order[c + 1])
             softmax(h, t, half, *now)
             if half == halves - 1:
+                for copy in tile_stores(h, t):
+                    copy.start()
                 parts = trunk_parts(h, t)
                 totals = parts if t == 0 else tuple(a + b for a, b in zip(totals, parts))
-                for copy in tile_stores(h, t):
-                    copy.start()
         shape = (sums.shape[1], sums.shape[3], HEAD_SIZE)
         sums[h, :, 0] = (totals[0] * scale).reshape(shape).astype(jnp.bfloat16)
         sums[h, :, 1] = totals[1].reshape(shape).astype(jnp.bfloat16)

time: 49.6 us -> 49.5 us (level)
  no operation moved by 1% of the time
where the time goes in v3:
time: 49.5 us; the launch traced here: 49 us
  Pallas kernels  24.1 us (49%)
  starting transfers between devices  12.7 us (26%)
  waiting for transfers between devices  7.77 us (16%)
  local copies, waits for them, and re-layouts  2.98 us (6%)
  other arithmetic  0.8 us (2%)
  between operations  0.68 us (1%)
    pallas_call x1, Pallas kernels, per_device(): pl.pallas_call(lambda *refs: score_kernel(*refs, tiles=tiles), in_specs=[...  11.6 us
    all_to_all x1, starting transfers between devices, per_device(): lax.all_to_all(spread, 'seq', 0, 0, tiled=True).reshape(trunk, 2 * width)  8.67 us
    pallas_call x1, Pallas kernels, per_device(): pl.pallas_call(lambda *refs: grad_kernel(*refs, tiles=tiles), in_specs=[h...  7.51 us
    all_to_all x1, waiting for transfers between devices, per_device(): lax.all_to_all(spread, 'seq', 0, 0, tiled=True).reshape(trunk, 2 * width)  5.08 us
    pallas_call x1, Pallas kernels, per_device(): pl.pallas_call(lambda *refs: local_kernel(*refs, tiles=tiles), in_specs=[...  4.92 us
    all_to_all x1, starting transfers between devices, per_device(): shares = lax.all_to_all(sums, 'seq', 0, 0, tiled=True)  4.04 us
    all_to_all x1, waiting for transfers between devices, per_device(): shares = lax.all_to_all(sums, 'seq', 0, 0, tiled=True)  2.69 us
    unnamed x2, local copies, waits for them, and re-layouts  1.51 us
  transfers between devices with their start and end apart: 2, of which 2 were waited for; matrix products, arithmetic and copies ran while one was open for 3% of the time, Pallas kernels for 25%

profile of v3, /device:TPU:64, one launch (start us, length us, event | category | flops | bytes accessed | tf_op | source)
XLA Modules:
  0.0 49.0 jit_solution(8648992669193536258)
XLA Ops:
  0.6 0.7 %pad_maximum_fusion = bf16[8,1024]{1,0:T(8,128)(2,1)S(1)} fusion(bf16[8,512]{1,0:T(8,128)(2,1)} %bitcast.20, bf16[8,512]{1,0:T(8,128)(2,1)} %bitcast.21), kind=kLoop, calls=%fused_computation.1 | loop fusion | flops 32768 | bytes 32768 | tf_op jit(solution)/shard_map/concatenate | solution.py:446
  1.3 0.9 %broadcast_in_dim.15 = bf16[32,8,1024]{2,1,0:T(8,128)(2,1)} broadcast(bf16[8,1024]{1,0:T(8,128)(2,1)S(1)} %pad_maximum_fusion), dimensions={1,2} | broadcast | bytes 540672 | tf_op jit(solution)/shard_map/broadcast_in_dim | solution.py:447
  2.2 8.7 %all-to-all-start = ((bf16[32,8,1024]{2,1,0:T(8,128)(2,1)}), bf16[32,8,1024]{2,1,0:T(8,128)(2,1)S(1)}, u32[]{:S(2)}, u32[]{:S(2)}) async-start(bf16[32,8,1024]{2,1,0:T(8,128)(2,1)} %broadcast_in_dim.15), calls=%async_computation | async-start | bytes 1048576 | tf_op jit(solution)/shard_map/all_to_all | solution.py:448
  10.9 0.8 %copy.13.refs_1_ = s32[8,4]{1,0:T(8,128)S(1)} copy(s32[8,4]{0,1:T(4,128)} %param.14) | data formatting | bytes 256 | tf_op args[6]
  11.6 0.8 %copy.14.refs_2_ = s32[8,4]{1,0:T(8,128)S(1)} copy(s32[8,4]{0,1:T(4,128)} %param.15) | data formatting | bytes 256 | tf_op args[7]
  12.4 4.9 %local.1 = (bf16[4,4,64,512]{3,2,1,0:T(8,128)(2,1)}, bf16[4,4,64,512]{3,2,1,0:T(8,128)(2,1)}, f32[4,4,80,512]{3,2,1,0:T(8,128)}) custom-call(bf16[256,4096]{1,0:T(8,128)(2,1)} %bitcast.12, bf16[256,4096]{1,0:T(8,128)(2,1)} %bitcast.15, bf16[256,512]{1,0:T(8,128)(2,1)} %bitcast.18, bf16[256,512]{1,0:T(8,128)(2,1)} %bitcast.25), custom_call_target="tpu_custom_call" | custom-call | flops 1342177280 | bytes 7340032 | tf_op jit(solution)/shard_map/local/pallas_call | solution.py:459
  17.3 5.1 %all-to-all-done = bf16[32,8,1024]{2,1,0:T(8,128)(2,1)S(1)} async-done(((bf16[32,8,1024]{2,1,0:T(8,128)(2,1)}), bf16[32,8,1024]{2,1,0:T(8,128)(2,1)S(1)}, u32[]{:S(2)}, u32[]{:S(2)}) %all-to-all-start) | async-done | bytes 524320 | tf_op jit(solution)/shard_map/all_to_all | solution.py:448
  22.4 11.6 %scores.1 = (bf16[32,2,8,512]{3,2,1,0:T(8,128)(2,1)}, bf16[18,256,512]{2,1,0:T(8,128)(2,1)}, f32[4,4,80,512]{3,2,1,0:T(8,128)}) custom-call(s32[1]{0:T(128)} %bitcast.3.refs_0_, s32[8,4]{1,0:T(8,128)S(1)} %copy.13.refs_1_, s32[8,4]{1,0:T(8,128)S(1)} %copy.14.refs_2_, bf16[256,4096]{1,0:T(8,128)(2,1)} %bitcast.13, bf16[256,4096]{1,0:T(8,128)(2,1)} %bitcast.16, ...), custom_call_target="tpu_custom_call" | custom-call | flops 2684354560 | bytes 12582912 | tf_op jit(solution)/shard_map/scores/pallas_call | solution.py:485
  34.1 4.0 %all-to-all-start.1 = ((bf16[32,2,8,512]{3,2,1,0:T(8,128)(2,1)}), bf16[32,2,8,512]{3,2,1,0:T(8,128)(2,1)S(1)}, u32[]{:S(2)}, u32[]{:S(2)}) async-start(bf16[32,2,8,512]{3,2,1,0:T(8,128)(2,1)} %get-tuple-element.22), calls=%async_computation.1 | async-start | bytes 1048576 | tf_op jit(solution)/shard_map/all_to_all | solution.py:514
  38.1 7.5 %grads.1 = (f32[256,4096]{1,0:T(8,128)}, f32[256,512]{1,0:T(8,128)}, f32[256,512]{1,0:T(8,128)}) custom-call(bf16[256,4096]{1,0:T(8,128)(2,1)} %bitcast.14, bf16[256,4096]{1,0:T(8,128)(2,1)} %bitcast.17, bf16[256,512]{1,0:T(8,128)(2,1)} %bitcast.19, bf16[18,256,512]{2,1,0:T(8,128)(2,1)} %get-tuple-element.15.refs_3_, ...), custom_call_target="tpu_custom_call" | custom-call | flops 1342177280 | bytes 16777216 | tf_op jit(solution)/shard_map/grads/pallas_call | solution.py:516
  45.6 2.7 %all-to-all-done.1 = bf16[32,2,8,512]{3,2,1,0:T(8,128)(2,1)S(1)} async-done(((bf16[32,2,8,512]{3,2,1,0:T(8,128)(2,1)}), bf16[32,2,8,512]{3,2,1,0:T(8,128)(2,1)S(1)}, u32[]{:S(2)}, u32[]{:S(2)}) %all-to-all-start.1) | async-done | bytes 524320 | tf_op jit(solution)/shard_map/all_to_all | solution.py:514
  48.3 0.1 convert_reduce_fusion
  48.4 0.6 %fusion = (f32[1,8,512]{2,1,0:T(8,128)}, f32[1,8,512]{2,1,0:T(8,128)}) fusion(f32[2,8,512]{2,1,0:T(8,128)S(1)} %convert_reduce_fusion), kind=kLoop, calls=%fused_computation.2 | loop fusion | bytes 65536 | tf_op jit(solution)/shard_map/slice | solution.py:546
Async XLA Ops:
  2.2 20.2 %all-to-all-start = ((bf16[32,8,1024]{2,1,0:T(8,128)(2,1)}), bf16[32,8,1024]{2,1,0:T(8,128)(2,1)S(1)}, u32[]{:S(2)}, u32[]{:S(2)}) async-start(bf16[32,8,1024]{2,1,0:T(8,128)(2,1)} %broadcast_in_dim.15), calls=%async_computation | async-start | bytes 1048576 | tf_op jit(solution)/shard_map/all_to_all | solution.py:448
  34.1 14.3 %all-to-all-start.1 = ((bf16[32,2,8,512]{3,2,1,0:T(8,128)(2,1)}), bf16[32,2,8,512]{3,2,1,0:T(8,128)(2,1)S(1)}, u32[]{:S(2)}, u32[]{:S(2)}) async-start(bf16[32,2,8,512]{3,2,1,0:T(8,128)(2,1)} %get-tuple-element.22), calls=%async_computation.1 | async-start | bytes 1048576 | tf_op jit(solution)/shard_map/all_to_all | solution.py:514
